TPU v7x, 32 devices: a whole 2x2x4 slice. The times are simulated.
32 devices in a mesh: a3: 4 (over z), a2: 2 (over y), a1: 4 (over x, core).
Axes of the slice: x: 2, y: 2, z: 4, core: 2. Of those that a mesh axis runs over, the one named last changes fastest.
Arguments:
- tensor: bfloat16 [384, 720, 1280], P('a1', 'a2', 'a3')
- u_time: float32 [384, 48], replicated
- u_height: float32 [720, 88], replicated
- u_width: float32 [1280, 160], replicated
Outputs:
- output 1: float32 [384, 48], replicated
- output 2: float32 [720, 88], replicated
- output 3: float32 [1280, 160], replicated
- output 4: float32 [48, 88, 160], P('a1', 'a2', 'a3')
- output 5: float32 [], replicated
All inputs are finite; a program needn't handle non-finite values.
Results may differ from a plain program's by a relative error of at most 0.00377637.
Values are sent between devices in bfloat16 or wider.
A program may use at most 1 GiB of HBM per device.

v0:
```python
import jax
import jax.numpy as jnp
from jax import lax
from jax.sharding import PartitionSpec as P


def rows_of(factor, axis_name, count):
    start_row = lax.axis_index(axis_name) * count
    return lax.dynamic_slice_in_dim(factor, start_row, count, 0).astype(jnp.bfloat16)


def gram_update(local_rows, row_axes, sum_axes, factor):
    all_rows = lax.all_gather(local_rows, row_axes, axis=0, tiled=True)
    gram_part = lax.dot_general(local_rows, all_rows, (((1,), (1,)), ((), ())), preferred_element_type=jnp.float32)
    gram_rows = lax.psum(gram_part, sum_axes).astype(jnp.bfloat16)
    power_cols = jnp.dot(gram_rows, factor.astype(jnp.bfloat16), preferred_element_type=jnp.float32)
    col_sq = lax.psum(jnp.sum(power_cols * power_cols, axis=0, keepdims=True), row_axes)
    return lax.all_gather(power_cols / jnp.sqrt(col_sq), row_axes, axis=0, tiled=True)


def solution(mesh):
    def local_sweep(tensor, u_time, u_height, u_width):
        frames, grid_h, grid_w = tensor.shape
        t_part = jnp.dot(tensor.reshape(frames * grid_h, grid_w), rows_of(u_width, 'a3', grid_w), preferred_element_type=jnp.float32)
        t_mat = lax.psum_scatter(t_part.reshape(frames, grid_h, -1), 'a3', scatter_dimension=2, tiled=True).astype(jnp.bfloat16)
        y1_part = jnp.einsum('ihc,hb->icb', t_mat, rows_of(u_height, 'a2', grid_h), preferred_element_type=jnp.float32)
        y_one = lax.psum_scatter(y1_part, 'a2', scatter_dimension=2, tiled=True).astype(jnp.bfloat16)
        new_time = gram_update(y_one.reshape(frames, -1), 'a1', ('a2', 'a3'), u_time)
        time_rows = rows_of(new_time, 'a1', frames)
        y2_part = jnp.einsum('ihc,ia->hca', t_mat, time_rows, preferred_element_type=jnp.float32)
        y_two = lax.psum_scatter(y2_part, 'a1', scatter_dimension=2, tiled=True).astype(jnp.bfloat16)
        new_height = gram_update(y_two.reshape(grid_h, -1), 'a2', ('a1', 'a3'), u_height)
        z_part = lax.dot_general(time_rows, tensor.reshape(frames, grid_h * grid_w), (((0,), (0,)), ((), ())), preferred_element_type=jnp.float32)
        z_mat = lax.psum_scatter(z_part, 'a1', scatter_dimension=0, tiled=True).astype(jnp.bfloat16).reshape(-1, grid_h, grid_w)
        y3_part = jnp.einsum('ahw,hb->wab', z_mat, rows_of(new_height, 'a2', grid_h), preferred_element_type=jnp.float32)
        y_three = lax.psum_scatter(y3_part, 'a2', scatter_dimension=2, tiled=True).astype(jnp.bfloat16)
        new_width = gram_update(y_three.reshape(grid_w, -1), 'a3', ('a1', 'a2'), u_width)
        core_part = jnp.einsum('wab,wc->abc', y_three, rows_of(new_width, 'a3', grid_w), preferred_element_type=jnp.float32)
        core_tensor = lax.psum_scatter(core_part, 'a3', scatter_dimension=2, tiled=True)
        core_energy = lax.psum(jnp.sum(core_tensor * core_tensor), ('a1', 'a2', 'a3'))
        return new_time, new_height, new_width, core_tensor, core_energy

    return jax.shard_map(local_sweep, mesh=mesh, in_specs=(P('a1', 'a2', 'a3'), P(), P(), P()), out_specs=(P(), P(), P(), P('a1', 'a2', 'a3'), P()), check_vma=False)
```

profile of v0, /device:TPU:0, one launch (start us, length us, event | category | flops | bytes accessed | tf_op | source)
XLA Modules:
  0.0 1448.7 jit_solution(15880802864106774273)
XLA Ops:
  7.2 30.6 %copy.20 = bf16[96,360,320]{1,0,2:T(8,128)(2,1)} copy(bf16[96,360,320]{1,2,0:T(8,128)(2,1)} %param.4) | data formatting | bytes 44236800 | tf_op args[0]
  37.8 45.0 %reshape.31 = bf16[34560,320]{0,1:T(8,128)(2,1)} reshape(bf16[96,360,320]{1,0,2:T(8,128)(2,1)} %copy.20) | data formatting | bytes 44236800 | tf_op jit(solution)/shard_map/reshape | solution.py:24
  82.8 14.7 %convolution_bitcast_fusion = f32[34560,160]{0,1:T(8,128)} fusion(bf16[34560,320]{0,1:T(8,128)(2,1)} %reshape.31, f32[1280,160]{0,1:T(8,128)} %param.7, s32[]{:T(128)S(6)} %select_n.11), kind=kOutput, calls=%fused_computation | convolution fusion | flops 3538944000 | bytes 44359684 | tf_op jit(solution)/shard_map/dot_general | solution.py:24
  97.5 32.8 %reshape.32 = f32[96,360,160]{1,0,2:T(8,128)} reshape(f32[34560,160]{0,1:T(8,128)} %convolution_bitcast_fusion) | data formatting | bytes 44236800 | tf_op jit(solution)/shard_map/reshape | solution.py:25
  130.4 391.4 %reduce-scatter.8.cloned.1.call-done = f32[96,360,40]{1,0,2:T(8,128)} async-done(((f32[96,360,160]{1,0,2:T(8,128)}), f32[96,360,40]{1,0,2:T(8,128)}) %reduce-scatter.8.cloned.1.call-update) | async-done | bytes 5529616 | tf_op jit(solution)/shard_map/reduce_scatter | solution.py:25
  521.8 4.2 fusion.3
  526.0 1.6 copy.22
  527.7 29.7 %reduce-scatter.10.cloned.1.call-done = f32[96,40,44]{0,1,2:T(8,128)} async-done(((f32[96,40,88]{0,1,2:T(8,128)}), f32[96,40,44]{0,1,2:T(8,128)}) %reduce-scatter.10.cloned.1.call-update) | async-done | bytes 675856 | tf_op jit(solution)/shard_map/reduce_scatter | solution.py:27
  557.4 1.2 convert_element_type.51
  558.7 0.2 reshape.33
  558.9 0.9 copy.24
  559.9 29.9 %copy.30 = bf16[96,360,320]{2,1,0:T(8,128)(2,1)} copy(bf16[96,360,320]{1,2,0:T(8,128)(2,1)} %param.4) | data formatting | bytes 44236800 | tf_op args[0]
  589.8 25.8 %reshape.35 = bf16[96,115200]{1,0:T(8,128)(2,1)} reshape(bf16[96,360,320]{2,1,0:T(8,128)(2,1)} %copy.30) | data formatting | bytes 44236800 | tf_op jit(solution)/shard_map/reshape | solution.py:33
  615.6 1.9 fusion.29
  617.5 39.1 %all-reduce.7 = bf16[96,384]{1,0:T(8,128)(2,1)S(1)} all-reduce(f32[96,384]{1,0:T(8,128)S(1)} %fusion.29), channel_id=1, replica_groups=mesh['a3'=4,'a2'=2,'a1'=4] {'a2','a3'}, use_global_device_ids=true, to_apply=%region_2.0 | all-reduce | flops 36864 | bytes 221184 | tf_op jit(solution)/shard_map/psum | solution.py:15
  656.6 0.2 multiply_reduce_fusion.3
  656.8 5.7 psum.50
  662.5 0.1 divide_bitcast_fusion.2
  662.6 5.3 all-gather
  668.0 0.1 reshape.39
  668.1 14.0 fusion.22
  682.1 251.6 %fusion = f32[16,115200]{1,0:T(8,128)} fusion(f32[48,115200]{1,0:T(8,128)} %fusion.22), kind=kCustom, calls=%all-reduce-scatter | all-reduce-scatter fusion | flops 7372801 | bytes 29491712
  933.7 5.5 slice
  939.2 3.1 collective-permute-start
  942.3 0.6 dynamic-slice.6
  943.5 0.6 dynamic-slice.2
  944.8 3.3 fusion.1
  948.0 2.5 copy.26
  950.6 64.1 %concatenate = bf16[28,115200]{1,0:T(8,128)(2,1)} concatenate(bf16[12,115200]{1,0:T(8,128)(2,1)} %collective-permute-done, f32[16,115200]{1,0:T(8,128)} %fusion), dimensions={0} | concatenate | bytes 16588800
  1014.8 5.4 dynamic-slice_convert_fusion
  1020.1 4.3 reshape.36
  1024.5 1.2 convert_element_type.55
  1025.7 0.8 copy.27
  1026.5 1.9 reshape.34
  1028.5 1.9 copy.28
  1030.4 8.2 all_gather.20
  1038.5 2.5 fusion.30
  1041.0 124.2 %all-reduce.8 = bf16[360,720]{1,0:T(8,128)(2,1)} all-reduce(f32[360,720]{1,0:T(8,128)} %fusion.30), channel_id=1, replica_groups=mesh['a3'=4,'a2'=2,'a1'=4] {'a1','a3'}, use_global_device_ids=true, to_apply=%region_6.0 | all-reduce | flops 259200 | bytes 1555200 | tf_op jit(solution)/shard_map/psum | solution.py:15
  1165.2 1.5 multiply_reduce_fusion.2
  1166.8 6.4 psum.52
  1173.1 0.1 divide_bitcast_fusion.1
  1173.2 6.5 all-gather.1
  1179.7 0.8 copy.29
  1180.5 1.9 reshape.41
  1182.4 2.9 convolution_bitcast_fusion.1
  1185.3 40.5 %all-reduce.9 = bf16[320,12,88]{0,2,1:T(8,128)(2,1)S(1)} all-reduce(f32[320,12,88]{0,2,1:T(8,128)} %convolution_bitcast_fusion.1), channel_id=6, replica_groups=mesh['a3'=4,'a2'=2,'a1'=4] {'a2'}, use_global_device_ids=true, to_apply=%region_10.0.clone | all-reduce | flops 337920 | bytes 2027520
  1225.8 0.1 dynamic-slice_convert_fusion.1
  1226.0 0.9 reshape.42
  1226.9 0.1 reshape.37
  1227.1 39.7 %all-gather.9.cloned.1.call-done = bf16[4,320,528]{1,2,0:T(8,128)(2,1)} async-done(((bf16[1,320,528]{1,2,0:T(8,128)(2,1)}), bf16[4,320,528]{1,2,0:T(8,128)(2,1)}) %all-gather.9.cloned.1.call-update) | async-done | bytes 1351696 | tf_op jit(solution)/shard_map/all_gather | solution.py:13
  1266.8 2.0 copy.32
  1268.8 2.1 reshape.43
  1271.0 2.2 fusion.31
  1273.1 70.0 %all-reduce.10 = bf16[320,1280]{1,0:T(8,128)(2,1)S(1)} all-reduce(f32[320,1280]{1,0:T(8,128)S(1)} %fusion.31), channel_id=1, replica_groups=mesh['a3'=4,'a2'=2,'a1'=4] {'a1','a2'}, use_global_device_ids=true, to_apply=%region_11.0 | all-reduce | flops 409600 | bytes 2457600 | tf_op jit(solution)/shard_map/psum | solution.py:15
  1343.1 1.7 multiply_reduce_fusion.1
  1344.8 9.7 psum.54
  1354.6 0.1 divide_bitcast_fusion
  1354.7 19.1 %all-gather.3 = f32[4,320,160]{1,2,0:T(8,128)S(1)} all-gather(f32[1,320,160]{1,2,0:T(8,128)S(1)} %divide_bitcast_fusion), channel_id=1, replica_groups=mesh['a3'=4,'a2'=2,'a1'=4] {'a3'}, dimensions={0}, use_global_device_ids=true | all-gather | bytes 1024000 | tf_op jit(solution)/shard_map/all_gather | solution.py:18
  1373.7 0.6 copy.33
  1374.4 0.6 reshape.45
  1375.0 1.5 fusion.12
  1376.5 24.9 %reduce-scatter.14.cloned.1.call-done = f32[12,44,40]{1,2,0:T(8,128)} async-done(((f32[12,44,160]{1,2,0:T(8,128)}), f32[12,44,40]{1,2,0:T(8,128)}) %reduce-scatter.14.cloned.1.call-update) | async-done | bytes 84496 | tf_op jit(solution)/shard_map/reduce_scatter | solution.py:39
  1401.4 1.6 multiply_reduce_fusion
  1403.0 38.9 %psum.55 = f32[]{:T(128)} all-reduce(f32[]{:T(128)} %multiply_reduce_fusion), channel_id=1, replica_groups=mesh['a3'=4,'a2'=2,'a1'=4] {'a1','a2','a3'}, use_global_device_ids=true, to_apply=%region_16.0 | all-reduce | flops 1 | bytes 8 | tf_op jit(solution)/shard_map/psum | solution.py:40
  (30 shorter events, 0.5 us)
Async XLA Ops:
  7.2 514.6 %reduce-scatter.8.cloned.1.call-start = ((), (), s32[]{:S(2)}) async-start(), calls=%async_computation.4 | async-start | bytes 29491200 | tf_op jit(solution)/shard_map/reduce_scatter | solution.py:25
  130.3 427.1 %reduce-scatter.10.cloned.1.call-start = ((), (), s32[]{:S(2)}) async-start(), calls=%async_computation.5 | async-start | bytes 2703360 | tf_op jit(solution)/shard_map/reduce_scatter | solution.py:27
  527.6 88.0 %all-gather.7.cloned.1.call-start = ((), (), s32[]{:S(2)}) async-start(), calls=%async_computation.6 | async-start | bytes 1720320 | tf_op jit(solution)/shard_map/all_gather | solution.py:13
  559.8 464.7 %reduce-scatter.12.cloned.1.call-start = ((), (), s32[]{:S(2)}) async-start(), calls=%async_computation.7 | async-start | bytes 3686400 | tf_op jit(solution)/shard_map/reduce_scatter | solution.py:31
  589.8 66.8 %copy-start.2 = (f32[384,48]{0,1:T(8,128)S(1)}, f32[384,48]{0,1:T(8,128)}, u32[]{:S(2)}) copy-start(f32[384,48]{0,1:T(8,128)} %param.5) | copy-start | bytes 221188
  668.1 276.7 %copy-start.1 = (f32[384,48]{0,1:T(8,128)}, f32[384,48]{0,1:T(8,128)S(1)}, u32[]{:S(2)}) copy-start(f32[384,48]{0,1:T(8,128)S(1)} %reshape.39) | copy-start | bytes 221188
  933.7 8.6 copy-start.3
  933.7 9.8 copy-start.4
  939.2 11.4 collective-permute-start
  950.6 316.2 %all-gather.9.cloned.1.call-start = ((), (), s32[]{:S(2)}) async-start(), calls=%async_computation.9 | async-start | bytes 2027520 | tf_op jit(solution)/shard_map/all_gather | solution.py:13
  1226.9 174.5 %reduce-scatter.14.cloned.1.call-start = ((), (), s32[]{:S(2)}) async-start(), calls=%async_computation.8 | async-start | bytes 1228800 | tf_op jit(solution)/shard_map/reduce_scatter | solution.py:39
  1375.0 66.9 %copy-start = (f32[1280,160]{0,1:T(8,128)}, f32[1280,160]{0,1:T(8,128)S(1)}, u32[]{:S(2)}) copy-start(f32[1280,160]{0,1:T(8,128)S(1)} %reshape.45) | copy-start | bytes 2457604
Sparse Core Ops, SparseCore 0:
  130.5 391.2 reduce-scatter.7
  527.7 29.6 reduce-scatter.9
  560.0 18.2 all-gather.6
  950.7 38.4 reduce-scatter.11
  1227.0 39.7 all-gather.8
  1376.6 24.7 reduce-scatter.13
where the time goes:
time: 1460 us; the launch traced here: 1450 us
  blocking collectives  625 us (43%)
  waiting for transfers between devices  486 us (33%)
  local copies, waits for them, and re-layouts  264 us (18%)
  matrix products  50.6 us (3%)
  between operations  15.6 us (1%)
    reduce_scatter x1, waiting for transfers between devices, local_sweep(): lax.psum_scatter(t_part.reshape(frames, grid_h, -1), 'a3', scatter_dimens...  391 us
    unnamed x2, blocking collectives  292 us
    psum x3, blocking collectives, gram_update(): gram_rows = lax.psum(gram_part, sum_axes).astype(jnp.bfloat16)  233 us
    unnamed x21, local copies, waits for them, and re-layouts  137 us
    reshape x1, local copies, waits for them, and re-layouts, local_sweep(): tensor.reshape(frames * grid_h, grid_w)  45 us
    all_gather x2, waiting for transfers between devices, gram_update(): all_rows = lax.all_gather(local_rows, row_axes, axis=0, tiled=True)  39.7 us
    psum x1, blocking collectives, local_sweep(): lax.psum(jnp.sum(core_tensor * core_tensor), ('a1', 'a2', 'a3'))  38.9 us
    reshape x1, local copies, waits for them, and re-layouts, local_sweep(): t_part.reshape(frames, grid_h, -1)  32.8 us
  transfers between devices with their start and end apart: 7, of which 4 were waited for; matrix products, arithmetic and copies ran while one was open for 9% of the time, Pallas kernels for 0%

commit v1 on v0

v1 whole, which is shorter than its diff:
```python
import functools

import jax
import jax.numpy as jnp
from jax import lax
from jax.experimental import pallas as pl
from jax.experimental.pallas import tpu as pltpu
from jax.sharding import PartitionSpec as P

MESH = pl.DeviceIdType.MESH
F32 = jnp.float32
BF16 = jnp.bfloat16
SIZE = {"z": 4, "y": 2, "x": 2, "c": 2}
ALL = ("z", "y", "x", "c")
LAG = 2
SLOTS = 4
ROWS = 96
STEP = 88


def place():
    a1 = lax.axis_index("a1")
    return {"z": lax.axis_index("a3"), "y": lax.axis_index("a2"), "x": a1 // 2, "c": lax.rem(a1, 2)}


def device(at):
    return (at["z"], at["y"], at["x"] * 2 + at["c"])


def member(at, group):
    index = 0
    for axis in group:
        index = index * SIZE[axis] + at[axis]
    return index


def moved(at, group, index):
    new = dict(at)
    for axis in reversed(group):
        new[axis] = lax.rem(index, SIZE[axis])
        index = index // SIZE[axis]
    return new


def total(group):
    count = 1
    for axis in group:
        count *= SIZE[axis]
    return count


def exchange(values, group, ident, gather=False):
    count = total(group)
    block = values.shape if gather else values.shape[1:]

    def kernel(src, dst, send, recv, own_sem):
        at = place()
        me = member(at, group)
        barrier = pltpu.get_barrier_semaphore()
        others = [lax.rem(me + step, count) for step in range(1, count)]
        for other in others:
            pl.semaphore_signal(barrier, inc=1, device_id=device(moved(at, group, other)), device_id_type=MESH)
        own = pltpu.make_async_copy(src if gather else src.at[me], dst.at[me], own_sem)
        own.start()
        pl.semaphore_wait(barrier, count - 1)
        copies = []
        for step, other in enumerate(others):
            copy = pltpu.make_async_remote_copy(
                src_ref=src if gather else src.at[other], dst_ref=dst.at[me],
                send_sem=send.at[step], recv_sem=recv.at[step],
                device_id=device(moved(at, group, other)), device_id_type=MESH)
            copy.start()
            copies.append(copy)
        own.wait()
        for copy in copies:
            copy.wait()

    return pl.pallas_call(
        kernel,
        out_shape=jax.ShapeDtypeStruct((count,) + tuple(block), values.dtype),
        in_specs=[pl.BlockSpec(memory_space=pltpu.VMEM)],
        out_specs=pl.BlockSpec(memory_space=pltpu.VMEM),
        scratch_shapes=[pltpu.SemaphoreType.DMA((count - 1,)), pltpu.SemaphoreType.DMA((count - 1,)), pltpu.SemaphoreType.DMA],
        compiler_params=pltpu.CompilerParams(collective_id=ident, has_side_effects=True, vmem_limit_bytes=48 * 1024 * 1024),
        name="exchange_" + "".join(group) + "_" + str(ident),
    )(values)


def width_kernel(x_hbm, u_ref, t_ref, x_all, x_vmem, s_up, r_up, s_dn, r_dn,
                 load_sem, ss_up, rs_up, ss_dn, rs_dn, free_up, free_dn, x_send, x_recv, own_sem):
    frames = x_hbm.shape[0]
    at = place()
    z = at["z"]
    me = at["x"] * 2 + at["c"]
    half = t_ref.shape[1]
    loads = []
    for part in range(frames // 8):
        rows = pl.ds(part * 8, 8)
        load = pltpu.make_async_copy(x_hbm.at[rows], x_vmem.at[rows], load_sem.at[part])
        load.start()
        loads.append(load)
    partners = []
    for flip in (1, 2, 3):
        new = dict(at)
        if flip & 1:
            new["c"] = 1 - at["c"]
        if flip & 2:
            new["x"] = 1 - at["x"]
        partners.append(new)
    barrier = pltpu.get_barrier_semaphore()
    for new in partners:
        pl.semaphore_signal(barrier, inc=1, device_id=device(new), device_id_type=MESH)

    @pl.when(z > 0)
    def _():
        pl.semaphore_signal(barrier, inc=1, device_id=device({**at, "z": z - 1}), device_id_type=MESH)

    @pl.when(z < 3)
    def _():
        pl.semaphore_signal(barrier, inc=1, device_id=device({**at, "z": z + 1}), device_id_type=MESH)

    pl.semaphore_wait(barrier, 3 + jnp.minimum(z, 1) + jnp.minimum(3 - z, 1))

    swaps = []
    for step, new in enumerate(partners):
        other = new["x"] * 2 + new["c"]
        swap = pltpu.make_async_remote_copy(
            src_ref=x_hbm.at[:, pl.ds(pl.multiple_of(other * STEP, 8), ROWS), :], dst_ref=x_all.at[me],
            send_sem=x_send.at[step], recv_sem=x_recv.at[step], device_id=device(new), device_id_type=MESH)
        swap.start()
        swaps.append(swap)

    @pl.when((z > 0) & (z < 3))
    def _():
        @pl.loop(0, frames)
        def _(frame):
            t_ref[frame] = jnp.zeros(t_ref.shape[1:], BF16)

    def stream(frame, first, last, toward, back, factor, sends, recvs, ss, rs, free):
        @pl.when((frame >= 0) & (frame < frames))
        def _():
            slot = lax.rem(frame, SLOTS)
            copy = pltpu.make_async_remote_copy(
                src_ref=sends.at[slot], dst_ref=recvs.at[slot], send_sem=ss.at[slot], recv_sem=rs.at[slot],
                device_id=device({**at, "z": toward}), device_id_type=MESH)
            part = lax.dot_general(factor, x_vmem[frame], (((1,), (1,)), ((), ())), preferred_element_type=F32)

            @pl.when((z != last) & (frame >= SLOTS))
            def _():
                copy.wait_send()
                pl.semaphore_wait(free, 1)

            sends[slot] = part

            @pl.when(z != first)
            def _():
                copy.wait_recv()
                sends[slot] += recvs[slot]

                @pl.when(frame + SLOTS < frames)
                def _():
                    pl.semaphore_signal(free, inc=1, device_id=device({**at, "z": back}), device_id_type=MESH)

            @pl.when(z != last)
            def _():
                copy.start()

            @pl.when(z == last)
            def _():
                t_ref[frame] = sends[slot].astype(BF16)

    above = jnp.minimum(z + 1, 3)
    below = jnp.maximum(z - 1, 0)
    lead = jnp.minimum(z, 3 - z)

    @pl.loop(0, frames + 3 * LAG)
    def _(step):
        newest = step - LAG * lead

        @pl.when((newest >= 0) & (newest < frames) & (lax.rem(newest, 8) == 0))
        def _():
            part = newest // 8
            rows = pl.ds(pl.multiple_of(part * 8, 8), 8)
            pltpu.make_async_copy(x_hbm.at[rows], x_vmem.at[rows], load_sem.at[part]).wait()

        stream(step - LAG * z, 0, 3, above, below, u_ref[half:], s_up, r_up, ss_up, rs_up, free_up)
        stream(step - LAG * (3 - z), 3, 0, below, above, u_ref[:half], s_dn, r_dn, ss_dn, rs_dn, free_dn)

    own = pltpu.make_async_copy(x_vmem.at[:, pl.ds(pl.multiple_of(me * STEP, 8), ROWS), :], x_all.at[me], own_sem)
    own.start()

    @pl.when(z < 3)
    def _():
        for slot in range(SLOTS):
            pltpu.make_async_remote_copy(
                src_ref=s_up.at[slot], dst_ref=r_up.at[slot], send_sem=ss_up.at[slot], recv_sem=rs_up.at[slot],
                device_id=device({**at, "z": above}), device_id_type=MESH).wait_send()

    @pl.when(z > 0)
    def _():
        for slot in range(SLOTS):
            pltpu.make_async_remote_copy(
                src_ref=s_dn.at[slot], dst_ref=r_dn.at[slot], send_sem=ss_dn.at[slot], recv_sem=rs_dn.at[slot],
                device_id=device({**at, "z": below}), device_id_type=MESH).wait_send()

    own.wait()
    for swap in swaps:
        swap.wait()


def width_product(tensor, factor_rows):
    frames, grid_h, grid_w = tensor.shape
    rank = factor_rows.shape[1]
    half = rank // 2
    link = pltpu.VMEM((SLOTS, half, grid_h), F32)
    any_space = pl.BlockSpec(memory_space=pl.ANY)
    vmem = pl.BlockSpec(memory_space=pltpu.VMEM)
    sems = pltpu.SemaphoreType.DMA
    return pl.pallas_call(
        width_kernel,
        out_shape=(jax.ShapeDtypeStruct((frames, half, grid_h), BF16),
                   jax.ShapeDtypeStruct((4, frames, ROWS, grid_w), BF16)),
        in_specs=[any_space, vmem],
        out_specs=(vmem, any_space),
        scratch_shapes=[pltpu.VMEM(tensor.shape, BF16), link, link, link, link,
                        sems((frames // 8,)), sems((SLOTS,)), sems((SLOTS,)), sems((SLOTS,)), sems((SLOTS,)),
                        pltpu.SemaphoreType.REGULAR, pltpu.SemaphoreType.REGULAR, sems((3,)), sems((3,)), sems],
        compiler_params=pltpu.CompilerParams(collective_id=1, has_side_effects=True, vmem_limit_bytes=60 * 1024 * 1024),
        name="width_product",
    )(tensor, factor_rows.T)


def time_kernel(u_ref, x_ref, z_ref, kron):
    @pl.when(pl.program_id(0) == 0)
    def _():
        shape = (u_ref.shape[1], kron.shape[1])
        picks = lax.broadcasted_iota(jnp.int32, shape, 1) // 8 == lax.broadcasted_iota(jnp.int32, shape, 0)
        spread = jnp.dot(u_ref[...], jnp.where(picks, 1.0, 0.0).astype(BF16), preferred_element_type=F32)
        same = lax.rem(lax.broadcasted_iota(jnp.int32, kron.shape, 0), 8) == lax.rem(lax.broadcasted_iota(jnp.int32, kron.shape, 1), 8)
        kron[...] = jnp.where(same, spread, 0.0).astype(BF16)

    for part in range(x_ref.shape[1] // 8):
        rows = slice(part * 8, part * 8 + 8)
        block = x_ref[:, rows, :]
        flat = block.reshape(block.shape[0] * 8, block.shape[2])
        out = jnp.dot(kron[...], flat, preferred_element_type=F32)
        z_ref[:, rows, :] = out.reshape(z_ref.shape[0], 8, out.shape[1]).astype(BF16)


def time_product(x_all, new_time):
    frames = x_all.shape[0] * x_all.shape[1]
    rows, grid_w = x_all.shape[2:]
    rank = new_time.shape[1]
    spread = jnp.repeat(new_time.astype(BF16).T, 8, axis=0)
    tile = 16
    return pl.pallas_call(
        time_kernel,
        grid=(rows // tile,),
        out_shape=jax.ShapeDtypeStruct((rank, rows, grid_w), BF16),
        in_specs=[pl.BlockSpec((rank * 8, frames), lambda i: (0, 0)),
                  pl.BlockSpec((frames, tile, grid_w), lambda i: (0, i, 0))],
        out_specs=pl.BlockSpec((rank, tile, grid_w), lambda i: (0, i, 0)),
        scratch_shapes=[pltpu.VMEM((rank * 8, frames * 8), BF16)],
        compiler_params=pltpu.CompilerParams(vmem_limit_bytes=60 * 1024 * 1024),
        name="time_product",
    )(spread, x_all.reshape(frames, rows, grid_w))


def height_kernel(u_ref, z_ref, y_ref):
    for a in range(z_ref.shape[1]):
        acc = None
        for s in range(z_ref.shape[0]):
            term = jnp.dot(u_ref[s], z_ref[s, a], preferred_element_type=F32)
            acc = term if acc is None else acc + term
        y_ref[a] = acc.astype(BF16)


def height_product(z_blocks, u_blocks):
    vmem = pl.BlockSpec(memory_space=pltpu.VMEM)
    return pl.pallas_call(
        height_kernel,
        out_shape=jax.ShapeDtypeStruct((z_blocks.shape[1], u_blocks.shape[1], z_blocks.shape[3]), BF16),
        in_specs=[vmem, vmem], out_specs=vmem,
        compiler_params=pltpu.CompilerParams(vmem_limit_bytes=48 * 1024 * 1024),
        name="height_product",
    )(u_blocks, z_blocks)


def normalise(power_cols):
    return power_cols / jnp.sqrt(jnp.sum(power_cols * power_cols, axis=0, keepdims=True))


def rows_of(factor, axis_name, count):
    return lax.dynamic_slice_in_dim(factor, lax.axis_index(axis_name) * count, count, 0).astype(BF16)


def solution(mesh):
    def local_sweep(tensor, u_time, u_height, u_width):
        frames, grid_h, grid_w = tensor.shape
        rank_t, rank_h, rank_w = u_time.shape[1], u_height.shape[1], u_width.shape[1]
        t_mat, x_all = width_product(tensor, rows_of(u_width, "a3", grid_w))

        y1_part = jnp.einsum("ich,hb->icb", t_mat, rows_of(u_height, "a2", grid_h), preferred_element_type=F32)
        y1_part = y1_part.reshape(frames, 2, -1).swapaxes(0, 1)
        y_one = exchange(y1_part, ("y",), 2).sum(0).astype(BF16)
        y_rows = exchange(y_one, ("x", "c"), 3, gather=True)
        gram = jnp.einsum("ik,rjk->irj", y_one, y_rows, preferred_element_type=F32).reshape(8, frames // 8, -1)
        gram = exchange(gram, ("z", "y"), 4).sum(0).astype(BF16)
        power = jnp.dot(gram, u_time.astype(BF16), preferred_element_type=F32)
        new_time = normalise(exchange(power, ("x", "c", "z", "y"), 5, gather=True).reshape(-1, rank_t))

        z_part = time_product(x_all, new_time)
        z_blocks = exchange(z_part.reshape(8, rank_t // 8, ROWS, grid_w), ("x", "c", "y"), 6)

        y2_part = jnp.einsum("ich,ia->ach", t_mat, rows_of(new_time, "a1", frames), preferred_element_type=F32)
        y2_part = y2_part.reshape(2, rank_t // 2, rank_w // 2, grid_h)
        y2_part = exchange(y2_part, ("c",), 7).sum(0).reshape(2, rank_t // 4, rank_w // 2, grid_h)
        y_two = exchange(y2_part, ("x",), 8).sum(0).astype(BF16).reshape(-1, grid_h)
        y_rows = exchange(y_two, ("y",), 9, gather=True)
        gram = jnp.einsum("kh,rkg->hrg", y_two, y_rows, preferred_element_type=F32).reshape(4, grid_h // 4, 2 * grid_h)
        gram = jnp.pad(gram, ((0, 0), (0, 6), (0, 0)))
        gram = exchange(gram, ("x", "c"), 10).sum(0).reshape(4, 24, 2 * grid_h)
        gram = exchange(gram, ("z",), 11).sum(0).astype(BF16)
        power = jnp.dot(gram, u_height.astype(BF16), preferred_element_type=F32)
        power = exchange(power, ("y", "x", "c", "z"), 12, gather=True)
        power = power.reshape(8, 96, rank_h)[:, :grid_h // 4].reshape(-1, rank_h)
        new_height = normalise(power)

        height_t = new_height.astype(BF16).T.reshape(rank_h, 2, grid_h)
        blocks = []
        for quarter in range(4):
            block = height_t[:, :, quarter * STEP:quarter * STEP + ROWS]
            if quarter < 3:
                block = jnp.where(jnp.arange(ROWS) < STEP, block, 0)
            blocks.append(block)
        u_blocks = jnp.stack(blocks).transpose(0, 2, 1, 3).reshape(8, rank_h, ROWS)
        y_three = height_product(z_blocks, u_blocks)
        y_flat = y_three.reshape(-1, grid_w)
        y_rows = exchange(y_flat, ("z",), 13, gather=True)
        gram = jnp.einsum("kw,rkv->wrv", y_flat, y_rows, preferred_element_type=F32).reshape(8, grid_w // 8, 4 * grid_w)
        gram = exchange(gram, ("y", "x", "c"), 14).sum(0).astype(BF16)
        power = jnp.dot(gram, u_width.astype(BF16), preferred_element_type=F32)
        power = exchange(power.reshape(-1, 128), ALL, 15, gather=True)
        new_width = normalise(power.reshape(-1, rank_w))

        core = jnp.dot(y_flat, rows_of(new_width, "a3", grid_w), preferred_element_type=F32)
        core = core.reshape(rank_t // 8, 2, rank_h // 2, 4, rank_w // 4).transpose(3, 1, 0, 2, 4)
        core = exchange(core.reshape(8, rank_t // 8, -1), ("z", "y"), 16)
        core = core.reshape(4, rank_t // 4, -1).sum(0)
        core_tensor = core.reshape(rank_t // 4, rank_h // 2, rank_w // 4)
        energy = jnp.full((8, 128), jnp.sum(core_tensor * core_tensor))
        core_energy = jnp.sum(exchange(energy, ALL, 17, gather=True)[:, 0, 0])
        return new_time, new_height, new_width, core_tensor, core_energy

    return jax.shard_map(local_sweep, mesh=mesh, in_specs=(P("a1", "a2", "a3"), P(), P(), P()), out_specs=(P(), P(), P(), P("a1", "a2", "a3"), P()), check_vma=False)
```

time: 1460 us -> 755 us (0.52)
  Pallas kernels: 0 us -> 669 us
  blocking collectives: 625 us -> 0 us
  waiting for transfers between devices: 486 us -> 0 us
  local copies, waits for them, and re-layouts: 264 us -> 59.4 us
  matrix products: 50.6 us -> 15.2 us
    pallas_call x0 -> x19, Pallas kernels: none -> 669 us  [the longest x16 337 us: exchange(): pl.pallas_call(kernel, out_shape=jax.ShapeDtypeStruct((count,) + tuple(bl...]
    reduce_scatter x4 -> x0, waiting for transfers between devices: 446 us -> none  [the longest x1 391 us: local_sweep(): lax.psum_scatter(t_part.reshape(frames, grid_h, -1), 'a3', scatter_dimens...]
    psum x7 -> x0, blocking collectives: 294 us -> none  [the longest x3 233 us: gram_update(): gram_rows = lax.psum(gram_part, sum_axes).astype(jnp.bfloat16)]
    unnamed x2 -> x0, blocking collectives: 292 us -> none
    reshape x9 -> x15, local copies, waits for them, and re-layouts: 113 us -> 9.32 us  [the longest x2 5.85 us: local_sweep(): y1_part = y1_part.reshape(frames, 2, -1).swapaxes(0, 1)]
    unnamed x21, local copies, waits for them, and re-layouts: 137 us -> 37.6 us
    all_gather x2 -> x0, waiting for transfers between devices: 39.7 us -> none  [gram_update(): all_rows = lax.all_gather(local_rows, row_axes, axis=0, tiled=True)]
    all_gather x4 -> x0, blocking collectives: 39 us -> none  [the longest x3 30.9 us: gram_update(): lax.all_gather(power_cols / jnp.sqrt(col_sq), row_axes, axis=0, tiled=True)]
  transfers between devices with their start and end apart: 7 -> 0, of which waited for: 4 -> 0; matrix products, arithmetic and copies ran while one was open for 9% -> 0% of each run, Pallas kernels for 0% -> 0%
where the time goes in v1:
time: 755 us; the launch traced here: 753 us
  Pallas kernels  669 us (89%)
  local copies, waits for them, and re-layouts  59.4 us (8%)
  matrix products  15.2 us (2%)
  other arithmetic  8.78 us (1%)
    pallas_call x16, Pallas kernels, exchange(): pl.pallas_call(kernel, out_shape=jax.ShapeDtypeStruct((count,) + tuple(bl...  337 us
    pallas_call x1, Pallas kernels, width_product(): pl.pallas_call(width_kernel, out_shape=(jax.ShapeDtypeStruct((frames, hal...  311 us
    unnamed x21, local copies, waits for them, and re-layouts  37.6 us
    pallas_call x1, Pallas kernels, time_product(): pl.pallas_call(time_kernel, grid=(rows // tile,), out_shape=jax.ShapeDtyp...  20.2 us

profile of v1, /device:TPU:0, one launch (start us, length us, event | category | flops | bytes accessed | tf_op | source)
XLA Modules:
  0.0 753.4 jit_solution(12050571599826348897)
XLA Ops:
  0.6 1.7 fusion.10.u_ref
  2.4 30.2 %copy.22.x_hbm = bf16[96,360,320]{2,1,0:T(8,128)(2,1)} copy(bf16[96,360,320]{1,2,0:T(8,128)(2,1)} %param.4) | data formatting | bytes 44236800 | tf_op args[0]
  32.6 310.9 %width_product.1 = (bf16[96,80,360]{2,1,0:T(8,128)(2,1)}, bf16[4,96,96,320]{3,2,1,0:T(8,128)(2,1)}) custom-call(bf16[96,360,320]{2,1,0:T(8,128)(2,1)} %copy.22.x_hbm, bf16[160,320]{1,0:T(8,128)(2,1)} %fusion.10.u_ref), custom_call_target="tpu_custom_call" | custom-call | tf_op jit(solution)/shard_map/width_product/pallas_call | solution.py:219
  343.5 6.4 fusion.13
  349.9 5.3 reshape.92
  355.2 0.5 copy.64
  355.8 33.1 %exchange_y_2.1 = f32[2,96,3520]{2,1,0:T(8,128)S(1)} custom-call(f32[2,96,3520]{2,1,0:T(8,128)S(1)} %bitcast.74), custom_call_target="tpu_custom_call" | custom-call | tf_op jit(solution)/shard_map/exchange_y_2/pallas_call | solution.py:78
  388.9 0.2 reduce_sum.117.src
  389.1 31.1 %exchange_xc_3.1 = bf16[4,96,3520]{2,1,0:T(8,128)(2,1)S(1)} custom-call(bf16[96,3520]{1,0:T(8,128)(2,1)S(1)} %reduce_sum.117.src), custom_call_target="tpu_custom_call" | custom-call | tf_op jit(solution)/shard_map/exchange_xc_3/pallas_call | solution.py:78
  420.3 1.1 fusion.2
  421.4 0.1 copy.24
  421.5 0.1 reshape.93.src
  421.7 9.5 %exchange_zy_4.1 = f32[8,12,384]{2,1,0:T(8,128)S(1)} custom-call(f32[8,12,384]{2,1,0:T(8,128)S(1)} %reshape.93.src), custom_call_target="tpu_custom_call" | custom-call | tf_op jit(solution)/shard_map/exchange_zy_4/pallas_call | solution.py:78
  431.2 0.1 fusion.19.src
  431.3 11.4 %exchange_xczy_5.1 = f32[32,12,48]{2,1,0:T(8,128)S(1)} custom-call(f32[12,48]{1,0:T(8,128)S(1)} %fusion.19.src), custom_call_target="tpu_custom_call" | custom-call | tf_op jit(solution)/shard_map/exchange_xczy_5/pallas_call | solution.py:78
  443.1 4.0 fusion
  447.0 4.3 copy.27
  451.3 8.4 %exchange_c_7.1 = f32[2,24,80,360]{3,2,1,0:T(8,128)S(1)} custom-call(f32[2,24,80,360]{3,2,1,0:T(8,128)} %bitcast.85), custom_call_target="tpu_custom_call" | custom-call | tf_op jit(solution)/shard_map/exchange_c_7/pallas_call | solution.py:78
  459.8 2.5 copy-done
  462.3 3.4 reduce_sum.120
  465.7 34.6 %exchange_x_8.1 = f32[2,12,80,360]{3,2,1,0:T(8,128)S(1)} custom-call(f32[2,12,80,360]{3,2,1,0:T(8,128)S(1)} %bitcast.73), custom_call_target="tpu_custom_call" | custom-call | tf_op jit(solution)/shard_map/exchange_x_8/pallas_call | solution.py:78
  500.3 1.7 copy-done.1
  502.0 2.1 reduce_sum.121
  504.1 17.9 %exchange_y_9.1 = bf16[2,960,360]{2,1,0:T(8,128)(2,1)S(1)} custom-call(bf16[960,360]{1,0:T(8,128)(2,1)S(1)} %bitcast.75), custom_call_target="tpu_custom_call" | custom-call | tf_op jit(solution)/shard_map/exchange_y_9/pallas_call | solution.py:78
  522.0 1.6 copy.29
  523.6 0.3 copy.28
  523.9 1.1 dot_general.54
  525.0 1.9 fusion.27
  527.1 14.7 %exchange_xc_10.1 = f32[4,96,720]{2,1,0:T(8,128)S(1)} custom-call(f32[4,96,720]{2,1,0:T(8,128)S(1)} %pad.4.src), custom_call_target="tpu_custom_call" | custom-call | tf_op jit(solution)/shard_map/exchange_xc_10/pallas_call | solution.py:78
  541.9 8.9 %exchange_z_11.1 = f32[4,24,720]{2,1,0:T(8,128)S(1)} custom-call(f32[4,24,720]{2,1,0:T(8,128)S(1)} %bitcast.82), custom_call_target="tpu_custom_call" | custom-call | tf_op jit(solution)/shard_map/exchange_z_11/pallas_call | solution.py:78
  550.8 0.1 fusion.8.src
  551.0 16.9 %exchange_yxcz_12.1 = f32[32,24,88]{2,1,0:T(8,128)S(1)} custom-call(f32[24,88]{1,0:T(8,128)S(1)} %fusion.8.src), custom_call_target="tpu_custom_call" | custom-call | tf_op jit(solution)/shard_map/exchange_yxcz_12/pallas_call | solution.py:78
  568.1 0.2 copy.44
  568.2 0.8 convert_bitcast_fusion
  569.0 0.2 reshape.100
  569.2 0.2 fusion.26
  569.5 0.7 broadcast_bitcast_fusion.u_ref
  570.3 20.2 %time_product.1 = bf16[48,96,320]{2,1,0:T(8,128)(2,1)} custom-call(bf16[384,384]{1,0:T(8,128)(2,1)} %broadcast_bitcast_fusion.u_ref, bf16[384,96,320]{2,1,0:T(8,128)(2,1)} %bitcast.84), custom_call_target="tpu_custom_call" | custom-call | tf_op jit(solution)/shard_map/time_product/pallas_call | solution.py:256
  590.4 43.6 %exchange_xcy_6.1.z_ref = bf16[8,6,96,320]{3,2,1,0:T(8,128)(2,1)S(1)} custom-call(bf16[8,6,96,320]{3,2,1,0:T(8,128)(2,1)} %bitcast.86), custom_call_target="tpu_custom_call" | custom-call | tf_op jit(solution)/shard_map/exchange_xcy_6/pallas_call | solution.py:78
  634.0 1.1 height_product.1
  635.1 30.2 %exchange_z_13.1 = bf16[4,528,320]{2,1,0:T(8,128)(2,1)S(1)} custom-call(bf16[528,320]{1,0:T(8,128)(2,1)S(1)} %bitcast.78), custom_call_target="tpu_custom_call" | custom-call | tf_op jit(solution)/shard_map/exchange_z_13/pallas_call | solution.py:78
  665.3 0.6 copy.36
  665.9 1.3 reshape.115
  667.2 0.2 copy.35
  667.4 0.8 fusion.28.src
  668.3 19.1 %exchange_yxc_14.1 = f32[8,40,1280]{2,1,0:T(8,128)S(1)} custom-call(f32[8,40,1280]{2,1,0:T(8,128)S(1)} %fusion.28.src), custom_call_target="tpu_custom_call" | custom-call | tf_op jit(solution)/shard_map/exchange_yxc_14/pallas_call | solution.py:78
  687.5 0.2 fusion.5
  687.7 0.1 reshape.106.src
  687.8 27.6 %exchange_zyxc_15.1 = f32[32,50,128]{2,1,0:T(8,128)S(1)} custom-call(f32[50,128]{1,0:T(8,128)S(1)} %reshape.106.src), custom_call_target="tpu_custom_call" | custom-call | tf_op jit(solution)/shard_map/exchange_zyxc_15/pallas_call | solution.py:78
  715.4 0.6 reshape.107
  716.0 0.2 multiply_reduce_fusion
  716.3 1.1 copy-done.2
  717.4 0.1 copy.37
  717.7 0.5 convolution_bitcast_fusion
  718.1 0.5 copy.45
  718.6 0.6 reshape.121.src
  719.3 17.1 %exchange_zy_16.1 = f32[8,6,1760]{2,1,0:T(8,128)S(1)} custom-call(f32[8,6,1760]{2,1,0:T(8,128)S(1)} %reshape.121.src), custom_call_target="tpu_custom_call" | custom-call | tf_op jit(solution)/shard_map/exchange_zy_16/pallas_call | solution.py:78
  736.5 0.2 reshape.110
  736.7 0.9 copy.41
  737.6 0.6 multiply_reduce_fusion.3
  738.2 0.6 broadcast_in_dim.28.src
  738.8 12.6 %exchange_zyxc_17.1 = f32[32,8,128]{2,1,0:T(8,128)S(1)} custom-call(f32[8,128]{1,0:T(8,128)S(1)} %broadcast_in_dim.28.src), custom_call_target="tpu_custom_call" | custom-call | tf_op jit(solution)/shard_map/exchange_zyxc_17/pallas_call | solution.py:78
  751.4 0.6 slice_reduce_fusion
  752.1 1.3 copy.40
  (37 shorter events, 1.2 us)
Async XLA Ops:
  420.2 10.9 %copy-start.8 = (f32[384,48]{0,1:T(8,128)S(1)}, f32[384,48]{0,1:T(8,128)}, u32[]{:S(2)}) copy-start(f32[384,48]{0,1:T(8,128)} %param.5) | copy-start | bytes 221188
  443.1 4.0 copy-start.7
  459.8 2.5 copy-start
  500.3 1.7 copy-start.1
  523.6 1.4 copy-start.4
  527.1 23.8 %copy-start.6 = (f32[720,88]{0,1:T(8,128)S(1)}, f32[720,88]{0,1:T(8,128)}, u32[]{:S(2)}) copy-start(f32[720,88]{0,1:T(8,128)} %param.6) | copy-start | bytes 760324
  668.3 19.2 %copy-start.5 = (f32[1280,160]{0,1:T(8,128)S(1)}, f32[1280,160]{0,1:T(8,128)}, u32[]{:S(2)}) copy-start(f32[1280,160]{0,1:T(8,128)} %param.7) | copy-start | bytes 2457604
  716.3 1.1 copy-start.2
  718.6 33.5 %copy-start.3 = (f32[1280,160]{1,0:T(8,128)S(1)}, f32[1280,160]{1,0:T(8,128)}, u32[]{:S(2)}) copy-start(f32[1280,160]{1,0:T(8,128)} %copy-done.2) | copy-start | bytes 2457604

commit v2 on v1

--- a/solution.py
+++ b/solution.py
@@ -14,8 +14,6 @@
 ALL = ("z", "y", "x", "c")
 LAG = 2
 SLOTS = 4
-ROWS = 96
-STEP = 88
 
 
 def place():
@@ -86,51 +84,49 @@
     )(values)
 
 
-def width_kernel(x_hbm, u_ref, t_ref, x_all, x_vmem, s_up, r_up, s_dn, r_dn,
-                 load_sem, ss_up, rs_up, ss_dn, rs_dn, free_up, free_dn, x_send, x_recv, own_sem):
+BATCH = 16
+
+
+def edge_member(at):
+    return ((at["x"] * 2 + at["c"]) * 2 + at["z"] // 3) * 2 + at["y"]
+
+
+def first_kernel(x_hbm, u3_ref, u2_ref, u1_ref, t_ref, x_all, new_ref, x_vmem, s_up, r_up, s_dn, r_dn,
+                 y_part, y_recv, y_all, g_part, g_recv, p_send, p_all,
+                 load_sem, ss_up, rs_up, ss_dn, rs_dn, free_up, free_dn, x_send, x_recv, own_sem,
+                 y_ss, y_rs, c_ss, c_rs, w_ss, w_rs, f_ss, f_rs, g_ss, g_rs, p_ss, p_rs):
     frames = x_hbm.shape[0]
     at = place()
     z = at["z"]
     me = at["x"] * 2 + at["c"]
     half = t_ref.shape[1]
-    loads = []
-    for part in range(frames // 8):
+    quarter = x_all.shape[2]
+    mine = member(at, ALL)
+    edge = (z == 0) | (z == 3)
+    loads = frames // 8
+    for part in range(loads):
         rows = pl.ds(part * 8, 8)
-        load = pltpu.make_async_copy(x_hbm.at[rows], x_vmem.at[rows], load_sem.at[part])
-        load.start()
-        loads.append(load)
-    partners = []
-    for flip in (1, 2, 3):
-        new = dict(at)
-        if flip & 1:
-            new["c"] = 1 - at["c"]
-        if flip & 2:
-            new["x"] = 1 - at["x"]
-        partners.append(new)
+        pltpu.make_async_copy(x_hbm.at[rows], x_vmem.at[rows], load_sem.at[part]).start()
     barrier = pltpu.get_barrier_semaphore()
-    for new in partners:
-        pl.semaphore_signal(barrier, inc=1, device_id=device(new), device_id_type=MESH)
-
-    @pl.when(z > 0)
-    def _():
-        pl.semaphore_signal(barrier, inc=1, device_id=device({**at, "z": z - 1}), device_id_type=MESH)
-
-    @pl.when(z < 3)
-    def _():
-        pl.semaphore_signal(barrier, inc=1, device_id=device({**at, "z": z + 1}), device_id_type=MESH)
-
-    pl.semaphore_wait(barrier, 3 + jnp.minimum(z, 1) + jnp.minimum(3 - z, 1))
-
+    for step in range(1, 32):
+        other = moved(at, ALL, lax.rem(mine + step, 32))
+        pl.semaphore_signal(barrier, inc=1, device_id=device(other), device_id_type=MESH)
+    pl.semaphore_wait(barrier, 31)
+
+    core_pair = {**at, "c": 1 - at["c"]}
+    x_pair = {**at, "x": 1 - at["x"]}
+    y_pair = {**at, "y": 1 - at["y"]}
+    partners = [core_pair, x_pair, {**core_pair, "x": 1 - at["x"]}]
     swaps = []
     for step, new in enumerate(partners):
         other = new["x"] * 2 + new["c"]
         swap = pltpu.make_async_remote_copy(
-            src_ref=x_hbm.at[:, pl.ds(pl.multiple_of(other * STEP, 8), ROWS), :], dst_ref=x_all.at[me],
+            src_ref=x_hbm.at[:, pl.ds(pl.multiple_of(other * quarter, 16), quarter), :], dst_ref=x_all.at[me],
             send_sem=x_send.at[step], recv_sem=x_recv.at[step], device_id=device(new), device_id_type=MESH)
         swap.start()
         swaps.append(swap)
 
-    @pl.when((z > 0) & (z < 3))
+    @pl.when(jnp.logical_not(edge))
     def _():
         @pl.loop(0, frames)
         def _(frame):
@@ -143,7 +139,7 @@
             copy = pltpu.make_async_remote_copy(
                 src_ref=sends.at[slot], dst_ref=recvs.at[slot], send_sem=ss.at[slot], recv_sem=rs.at[slot],
                 device_id=device({**at, "z": toward}), device_id_type=MESH)
-            part = lax.dot_general(factor, x_vmem[frame], (((1,), (1,)), ((), ())), preferred_element_type=F32)
+            part = jnp.dot(factor, x_vmem[frame], preferred_element_type=F32)
 
             @pl.when((z != last) & (frame >= SLOTS))
             def _():
@@ -167,7 +163,40 @@
 
             @pl.when(z == last)
             def _():
-                t_ref[frame] = sends[slot].astype(BF16)
+                done = sends[slot].astype(BF16)
+                t_ref[frame] = done
+                rows = jnp.dot(done, u2_ref[...], preferred_element_type=F32)
+                y_part[:, pl.ds(frame, 1), :] = rows[:, None, :]
+
+    keep = pl.ds(at["y"] * (half // 2), half // 2)
+    give = pl.ds((1 - at["y"]) * (half // 2), half // 2)
+
+    def rows_at(batch):
+        return pl.ds(pl.multiple_of(batch * BATCH, BATCH), BATCH)
+
+    def y_copy(batch):
+        return pltpu.make_async_remote_copy(
+            src_ref=y_part.at[give, rows_at(batch), :], dst_ref=y_recv.at[:, rows_at(batch), :],
+            send_sem=y_ss.at[batch], recv_sem=y_rs.at[batch], device_id=device(y_pair), device_id_type=MESH)
+
+    def spread_copy(owner, batch, pair, ss, rs):
+        block = y_all.at[owner, :, rows_at(batch), :]
+        return pltpu.make_async_remote_copy(
+            src_ref=block, dst_ref=block, send_sem=ss.at[batch], recv_sem=rs.at[batch],
+            device_id=device(pair), device_id_type=MESH)
+
+    far = x_pair["x"] * 2 + at["c"]
+
+    def settle(batch):
+        y_copy(batch).wait_recv()
+        rows = rows_at(batch)
+        y_all[me, :, rows, :] = (y_part[keep, rows, :] + y_recv[:, rows, :]).astype(BF16)
+        spread_copy(me, batch, core_pair, c_ss, c_rs).start()
+        spread_copy(me, batch, x_pair, w_ss, w_rs).start()
+
+    def forward(batch):
+        spread_copy(me, batch, x_pair, w_ss, w_rs).wait_recv()
+        spread_copy(far, batch, core_pair, f_ss, f_rs).start()
 
     above = jnp.minimum(z + 1, 3)
     below = jnp.maximum(z - 1, 0)
@@ -183,11 +212,109 @@
             rows = pl.ds(pl.multiple_of(part * 8, 8), 8)
             pltpu.make_async_copy(x_hbm.at[rows], x_vmem.at[rows], load_sem.at[part]).wait()
 
-        stream(step - LAG * z, 0, 3, above, below, u_ref[half:], s_up, r_up, ss_up, rs_up, free_up)
-        stream(step - LAG * (3 - z), 3, 0, below, above, u_ref[:half], s_dn, r_dn, ss_dn, rs_dn, free_dn)
-
-    own = pltpu.make_async_copy(x_vmem.at[:, pl.ds(pl.multiple_of(me * STEP, 8), ROWS), :], x_all.at[me], own_sem)
+        stream(step - LAG * z, 0, 3, above, below, u3_ref[half:], s_up, r_up, ss_up, rs_up, free_up)
+        stream(step - LAG * (3 - z), 3, 0, below, above, u3_ref[:half], s_dn, r_dn, ss_dn, rs_dn, free_dn)
+        final = step - 3 * LAG
+
+        @pl.when(edge & (final >= 0))
+        def _():
+            place_in = lax.rem(final, BATCH)
+            batch = final // BATCH
+
+            @pl.when(place_in == BATCH - 1)
+            def _():
+                y_copy(batch).start()
+
+            @pl.when((place_in == BATCH // 2) & (batch >= 1))
+            def _():
+                settle(batch - 1)
+
+            @pl.when((place_in == BATCH // 2) & (batch >= 2))
+            def _():
+                forward(batch - 2)
+
+    own = pltpu.make_async_copy(x_vmem.at[:, pl.ds(pl.multiple_of(me * quarter, 16), quarter), :], x_all.at[me], own_sem)
     own.start()
+    batches = frames // BATCH
+    last_batch = batches - 1
+
+    j = (z // 3) * 2 + at["y"]
+    piece = frames // 4
+    quads = []
+    for flip in (1, 2, 3):
+        new = dict(at)
+        if flip & 1:
+            new["y"] = 1 - at["y"]
+        if flip & 2:
+            new["z"] = 3 - z
+        quads.append(new)
+
+    def g_copy(step, new):
+        to = (new["z"] // 3) * 2 + new["y"]
+        return pltpu.make_async_remote_copy(
+            src_ref=g_part.at[:, pl.ds(pl.multiple_of(to * piece, 8), piece), :], dst_ref=g_recv.at[step],
+            send_sem=g_ss.at[step], recv_sem=g_rs.at[step], device_id=device(new), device_id_type=MESH)
+
+    slot16 = edge_member(at)
+
+    def p_copy(step):
+        other = moved(at, ALL, lax.rem(mine + step, 32))
+        return pltpu.make_async_remote_copy(
+            src_ref=p_send, dst_ref=p_all.at[slot16], send_sem=p_ss.at[step - 1], recv_sem=p_rs.at[slot16],
+            device_id=device(other), device_id_type=MESH)
+
+    @pl.when(edge)
+    def _():
+        settle(last_batch)
+        forward(last_batch - 1)
+        forward(last_batch)
+        for batch in range(batches):
+            spread_copy(me, batch, core_pair, c_ss, c_rs).wait_recv()
+            spread_copy(far, batch, core_pair, f_ss, f_rs).wait_recv()
+        g_part[...] = jnp.zeros(g_part.shape, F32)
+
+        @pl.loop(0, half // 2)
+        def _(col):
+            left = y_all[me, col]
+            for r in range(4):
+                g_part[r] += lax.dot_general(left, y_all[r, col], (((1,), (1,)), ((), ())), preferred_element_type=F32)
+
+        for step, new in enumerate(quads):
+            g_copy(step, new).start()
+        rows = pl.ds(pl.multiple_of(j * piece, 8), piece)
+        for step, new in enumerate(quads):
+            g_copy(step, new).wait_recv()
+        power = None
+        for r in range(4):
+            gram = g_part[r, rows, :] + g_recv[0, r] + g_recv[1, r] + g_recv[2, r]
+            term = jnp.dot(gram.astype(BF16), u1_ref[r], preferred_element_type=F32)
+            power = term if power is None else power + term
+        p_send[...] = power
+        p_all[slot16] = power
+        for step in range(1, 32):
+            p_copy(step).start()
+        for step, new in enumerate(quads):
+            g_copy(step, new).wait_send()
+        for batch in range(batches):
+            y_copy(batch).wait_send()
+            spread_copy(me, batch, core_pair, c_ss, c_rs).wait_send()
+            spread_copy(me, batch, x_pair, w_ss, w_rs).wait_send()
+            spread_copy(far, batch, core_pair, f_ss, f_rs).wait_send()
+
+    for source in range(16):
+        @pl.when(jnp.logical_not(edge) | (slot16 != source))
+        def _():
+            pltpu.make_async_remote_copy(
+                src_ref=p_send, dst_ref=p_all.at[source], send_sem=p_ss.at[0], recv_sem=p_rs.at[source],
+                device_id=device(moved(at, ALL, lax.rem(mine + 1, 32))), device_id_type=MESH).wait_recv()
+
+    squares = jnp.sum(jnp.sum(p_all[...] * p_all[...], axis=0), axis=0, keepdims=True)
+    new_ref[...] = p_all[...] / jnp.sqrt(squares)[None]
+
+    @pl.when(edge)
+    def _():
+        for step in range(1, 32):
+            p_copy(step).wait_send()
 
     @pl.when(z < 3)
     def _():
@@ -208,26 +335,36 @@
         swap.wait()
 
 
-def width_product(tensor, factor_rows):
-    frames, grid_h, grid_w = tensor.shape
-    rank = factor_rows.shape[1]
-    half = rank // 2
+def first_stage(tensor_t, u3_rows, u2_rows, u1):
+    frames, grid_w, grid_h = tensor_t.shape
+    half, rank_h, rank_t = u3_rows.shape[1] // 2, u2_rows.shape[1], u1.shape[1]
     link = pltpu.VMEM((SLOTS, half, grid_h), F32)
     any_space = pl.BlockSpec(memory_space=pl.ANY)
     vmem = pl.BlockSpec(memory_space=pltpu.VMEM)
     sems = pltpu.SemaphoreType.DMA
+    regular = pltpu.SemaphoreType.REGULAR
+    batches = frames // BATCH
+    piece = frames // 4
     return pl.pallas_call(
-        width_kernel,
+        first_kernel,
         out_shape=(jax.ShapeDtypeStruct((frames, half, grid_h), BF16),
-                   jax.ShapeDtypeStruct((4, frames, ROWS, grid_w), BF16)),
-        in_specs=[any_space, vmem],
-        out_specs=(vmem, any_space),
-        scratch_shapes=[pltpu.VMEM(tensor.shape, BF16), link, link, link, link,
+                   jax.ShapeDtypeStruct((4, frames, grid_w // 4, grid_h), BF16),
+                   jax.ShapeDtypeStruct((16, piece, rank_t), F32)),
+        in_specs=[any_space, vmem, vmem, vmem],
+        out_specs=(vmem, any_space, vmem),
+        scratch_shapes=[pltpu.VMEM(tensor_t.shape, BF16), link, link, link, link,
+                        pltpu.VMEM((half, frames, rank_h), F32), pltpu.VMEM((half // 2, frames, rank_h), F32),
+                        pltpu.VMEM((4, half // 2, frames, rank_h), BF16),
+                        pltpu.VMEM((4, frames, frames), F32), pltpu.VMEM((3, 4, piece, frames), F32),
+                        pltpu.VMEM((piece, rank_t), F32), pltpu.VMEM((16, piece, rank_t), F32),
                         sems((frames // 8,)), sems((SLOTS,)), sems((SLOTS,)), sems((SLOTS,)), sems((SLOTS,)),
-                        pltpu.SemaphoreType.REGULAR, pltpu.SemaphoreType.REGULAR, sems((3,)), sems((3,)), sems],
+                        regular, regular, sems((3,)), sems((3,)), sems,
+                        sems((batches,)), sems((batches,)), sems((batches,)), sems((batches,)),
+                        sems((batches,)), sems((batches,)), sems((batches,)), sems((batches,)),
+                        sems((3,)), sems((3,)), sems((31,)), sems((16,))],
         compiler_params=pltpu.CompilerParams(collective_id=1, has_side_effects=True, vmem_limit_bytes=60 * 1024 * 1024),
-        name="width_product",
-    )(tensor, factor_rows.T)
+        name="first_stage",
+    )(tensor_t, u3_rows.T, u2_rows, u1.astype(BF16).reshape(4, frames, rank_t))
 
 
 def time_kernel(u_ref, x_ref, z_ref, kron):
@@ -267,19 +404,21 @@
 
 
 def height_kernel(u_ref, z_ref, y_ref):
-    for a in range(z_ref.shape[1]):
-        acc = None
+    for group in range(y_ref.shape[0]):
+        block = None
         for s in range(z_ref.shape[0]):
-            term = jnp.dot(u_ref[s], z_ref[s, a], preferred_element_type=F32)
-            acc = term if acc is None else acc + term
-        y_ref[a] = acc.astype(BF16)
+            flat = z_ref[s, group].reshape(-1, z_ref.shape[-1])
+            term = jnp.dot(flat, u_ref[s], preferred_element_type=F32)
+            block = term if block is None else block + term
+        y_ref[group] = block.astype(BF16)
 
 
 def height_product(z_blocks, u_blocks):
     vmem = pl.BlockSpec(memory_space=pltpu.VMEM)
+    _, groups, many, width, _ = z_blocks.shape
     return pl.pallas_call(
         height_kernel,
-        out_shape=jax.ShapeDtypeStruct((z_blocks.shape[1], u_blocks.shape[1], z_blocks.shape[3]), BF16),
+        out_shape=jax.ShapeDtypeStruct((groups, many * width, u_blocks.shape[2]), BF16),
         in_specs=[vmem, vmem], out_specs=vmem,
         compiler_params=pltpu.CompilerParams(vmem_limit_bytes=48 * 1024 * 1024),
         name="height_product",
@@ -298,19 +437,12 @@
     def local_sweep(tensor, u_time, u_height, u_width):
         frames, grid_h, grid_w = tensor.shape
         rank_t, rank_h, rank_w = u_time.shape[1], u_height.shape[1], u_width.shape[1]
-        t_mat, x_all = width_product(tensor, rows_of(u_width, "a3", grid_w))
-
-        y1_part = jnp.einsum("ich,hb->icb", t_mat, rows_of(u_height, "a2", grid_h), preferred_element_type=F32)
-        y1_part = y1_part.reshape(frames, 2, -1).swapaxes(0, 1)
-        y_one = exchange(y1_part, ("y",), 2).sum(0).astype(BF16)
-        y_rows = exchange(y_one, ("x", "c"), 3, gather=True)
-        gram = jnp.einsum("ik,rjk->irj", y_one, y_rows, preferred_element_type=F32).reshape(8, frames // 8, -1)
-        gram = exchange(gram, ("z", "y"), 4).sum(0).astype(BF16)
-        power = jnp.dot(gram, u_time.astype(BF16), preferred_element_type=F32)
-        new_time = normalise(exchange(power, ("x", "c", "z", "y"), 5, gather=True).reshape(-1, rank_t))
-
-        z_part = time_product(x_all, new_time)
-        z_blocks = exchange(z_part.reshape(8, rank_t // 8, ROWS, grid_w), ("x", "c", "y"), 6)
+        t_mat, x_all, new_time = first_stage(tensor.swapaxes(1, 2), rows_of(u_width, "a3", grid_w), rows_of(u_height, "a2", grid_h), u_time)
+        new_time = new_time.reshape(-1, rank_t)
+
+        ordered = new_time.reshape(-1, 4, 2, rank_t // 8).swapaxes(1, 2).reshape(-1, rank_t)
+        z_part = time_product(x_all, ordered)
+        z_blocks = exchange(z_part.reshape(2, rank_t // 2, grid_w // 4, grid_h), ("y",), 6)
 
         y2_part = jnp.einsum("ich,ia->ach", t_mat, rows_of(new_time, "a1", frames), preferred_element_type=F32)
         y2_part = y2_part.reshape(2, rank_t // 2, rank_w // 2, grid_h)
@@ -326,16 +458,10 @@
         power = power.reshape(8, 96, rank_h)[:, :grid_h // 4].reshape(-1, rank_h)
         new_height = normalise(power)
 
-        height_t = new_height.astype(BF16).T.reshape(rank_h, 2, grid_h)
-        blocks = []
-        for quarter in range(4):
-            block = height_t[:, :, quarter * STEP:quarter * STEP + ROWS]
-            if quarter < 3:
-                block = jnp.where(jnp.arange(ROWS) < STEP, block, 0)
-            blocks.append(block)
-        u_blocks = jnp.stack(blocks).transpose(0, 2, 1, 3).reshape(8, rank_h, ROWS)
-        y_three = height_product(z_blocks, u_blocks)
-        y_flat = y_three.reshape(-1, grid_w)
+        u_blocks = new_height.astype(BF16).reshape(2, grid_h, rank_h)
+        y_three = height_product(z_blocks.reshape(2, 4, rank_t // 8, grid_w // 4, grid_h), u_blocks)
+        y_three = exchange(y_three, ("x", "c"), 2).reshape(4, rank_t // 8, grid_w // 4, rank_h)
+        y_flat = y_three.transpose(1, 3, 0, 2).reshape(-1, grid_w)
         y_rows = exchange(y_flat, ("z",), 13, gather=True)
         gram = jnp.einsum("kw,rkv->wrv", y_flat, y_rows, preferred_element_type=F32).reshape(8, grid_w // 8, 4 * grid_w)
         gram = exchange(gram, ("y", "x", "c"), 14).sum(0).astype(BF16)

time: 755 us -> 777 us (1.029)
  Pallas kernels: 669 us -> 711 us
  local copies, waits for them, and re-layouts: 59.4 us -> 42.6 us
    pallas_call x2, Pallas kernels: 312 us -> 441 us  [the longest x1 441 us: first_stage(): pl.pallas_call(first_kernel, out_shape=(jax.ShapeDtypeStruct((frames, hal...]
    pallas_call x16 -> x13, Pallas kernels: 337 us -> 252 us  [exchange(): pl.pallas_call(kernel, out_shape=jax.ShapeDtypeStruct((count,) + tuple(bl...]
    unnamed x21 -> x25, local copies, waits for them, and re-layouts: 37.6 us -> 15.1 us
where the time goes in v2:
time: 777 us
  Pallas kernels  711 us (92%)
  local copies, waits for them, and re-layouts  42.6 us (5%)
  other arithmetic  13.1 us (2%)
  matrix products  8.96 us (1%)
    pallas_call x1, Pallas kernels, first_stage(): pl.pallas_call(first_kernel, out_shape=(jax.ShapeDtypeStruct((frames, hal...  441 us
    pallas_call x13, Pallas kernels, exchange(): pl.pallas_call(kernel, out_shape=jax.ShapeDtypeStruct((count,) + tuple(bl...  252 us
    pallas_call x1, Pallas kernels, time_product(): pl.pallas_call(time_kernel, grid=(rows // tile,), out_shape=jax.ShapeDtyp...  17.7 us

profile of v2, /device:TPU:0, one launch (start us, length us, event | category | flops | bytes accessed | tf_op | source)
XLA Modules:
  0.0 776.5 jit_solution(10521530083182702772)
XLA Ops:
  0.6 0.9 convert_element_type.54
  1.5 0.8 copy.41
  2.3 1.0 constant_dynamic-slice_fusion
  3.3 0.7 copy.65.u2_ref
  4.0 1.7 fusion.8.u3_ref
  5.8 440.6 %first_stage.1 = (bf16[96,80,360]{2,1,0:T(8,128)(2,1)}, bf16[4,96,80,360]{3,2,1,0:T(8,128)(2,1)}, f32[16,24,48]{2,1,0:T(8,128)}) custom-call(bf16[96,320,360]{2,1,0:T(8,128)(2,1)} %bitcast.73, bf16[160,320]{1,0:T(8,128)(2,1)} %fusion.8.u3_ref, bf16[360,88]{1,0:T(8,128)(2,1)} %copy.65.u2_ref, bf16[4,96,48]{2,1,0:T(8,128)(2,1)} %bitcast.81), custom_call_target="tpu_custom_call" | custom-call | tf_op jit(solution)/shard_map/first_stage/pallas_call | solution.py:348
  446.3 1.0 copy.58
  447.4 4.0 fusion
  451.3 4.3 copy.44
  455.6 8.1 %exchange_c_7.1 = f32[2,24,80,360]{3,2,1,0:T(8,128)S(1)} custom-call(f32[2,24,80,360]{3,2,1,0:T(8,128)} %bitcast.74), custom_call_target="tpu_custom_call" | custom-call | tf_op jit(solution)/shard_map/exchange_c_7/pallas_call | solution.py:76
  463.7 2.5 copy-done
  466.2 3.4 reduce_sum.90
  469.6 34.5 %exchange_x_8.1 = f32[2,12,80,360]{3,2,1,0:T(8,128)S(1)} custom-call(f32[2,12,80,360]{3,2,1,0:T(8,128)S(1)} %bitcast.63), custom_call_target="tpu_custom_call" | custom-call | tf_op jit(solution)/shard_map/exchange_x_8/pallas_call | solution.py:76
  504.1 1.6 copy-done.2
  505.8 3.1 reduce_sum.91
  509.2 0.2 convert_element_type.62
  509.4 0.7 broadcast_bitcast_fusion.u_ref
  510.2 17.7 %time_product.1 = bf16[48,80,360]{2,1,0:T(8,128)(2,1)} custom-call(bf16[384,384]{1,0:T(8,128)(2,1)} %broadcast_bitcast_fusion.u_ref, bf16[384,80,360]{2,1,0:T(8,128)(2,1)} %bitcast.72), custom_call_target="tpu_custom_call" | custom-call | tf_op jit(solution)/shard_map/time_product/pallas_call | solution.py:393
  527.9 1.8 copy-done.1
  529.7 33.6 %exchange_y_6.1 = bf16[2,24,80,360]{3,2,1,0:T(8,128)(2,1)S(1)} custom-call(bf16[2,24,80,360]{3,2,1,0:T(8,128)(2,1)S(1)} %bitcast.61), custom_call_target="tpu_custom_call" | custom-call | tf_op jit(solution)/shard_map/exchange_y_6/pallas_call | solution.py:76
  563.4 2.3 copy.45
  565.6 2.2 dot_general.42
  567.9 1.1 copy-done.3
  569.0 17.2 %exchange_y_9.1 = bf16[2,960,360]{2,1,0:T(8,128)(2,1)S(1)} custom-call(bf16[960,360]{1,0:T(8,128)(2,1)S(1)} %bitcast.65), custom_call_target="tpu_custom_call" | custom-call | tf_op jit(solution)/shard_map/exchange_y_9/pallas_call | solution.py:76
  586.2 1.1 copy-done.4
  587.3 2.6 copy.46
  589.9 2.4 fusion.14
  592.4 14.4 %exchange_xc_10.1 = f32[4,96,720]{2,1,0:T(8,128)S(1)} custom-call(f32[4,96,720]{2,1,0:T(8,128)S(1)} %pad.4.src), custom_call_target="tpu_custom_call" | custom-call | tf_op jit(solution)/shard_map/exchange_xc_10/pallas_call | solution.py:76
  606.8 1.0 copy-done.5
  607.8 1.4 reduce_sum.92
  609.2 11.0 %exchange_z_11.1 = f32[4,24,720]{2,1,0:T(8,128)S(1)} custom-call(f32[4,24,720]{2,1,0:T(8,128)S(1)} %bitcast.71), custom_call_target="tpu_custom_call" | custom-call | tf_op jit(solution)/shard_map/exchange_z_11/pallas_call | solution.py:76
  620.3 1.1 fusion.6.src
  621.4 17.3 %exchange_yxcz_12.1 = f32[32,24,88]{2,1,0:T(8,128)S(1)} custom-call(f32[24,88]{1,0:T(8,128)S(1)} %fusion.6.src), custom_call_target="tpu_custom_call" | custom-call | tf_op jit(solution)/shard_map/exchange_yxcz_12/pallas_call | solution.py:76
  638.7 0.9 copy.66
  639.6 1.7 multiply_reduce_fusion.1
  641.3 2.0 reshape.104
  643.4 1.1 reshape.103
  644.5 0.8 broadcast_divide_fusion.1
  645.3 1.1 copy.48
  646.5 0.9 height_product.1.src
  647.4 7.2 exchange_xc_2.1
  654.6 0.3 copy.52
  654.9 0.3 reshape.110.src
  655.3 1.2 reshape.119
  656.5 0.2 copy.53
  656.7 30.9 %exchange_z_13.1 = bf16[4,528,320]{2,1,0:T(8,128)(2,1)S(1)} custom-call(bf16[528,320]{1,0:T(8,128)(2,1)S(1)} %reshape.110.src), custom_call_target="tpu_custom_call" | custom-call | tf_op jit(solution)/shard_map/exchange_z_13/pallas_call | solution.py:76
  687.6 0.6 copy.54
  688.3 1.5 reshape.118
  689.8 0.8 fusion.15.src
  690.6 19.6 %exchange_yxc_14.1 = f32[8,40,1280]{2,1,0:T(8,128)S(1)} custom-call(f32[8,40,1280]{2,1,0:T(8,128)S(1)} %fusion.15.src), custom_call_target="tpu_custom_call" | custom-call | tf_op jit(solution)/shard_map/exchange_yxc_14/pallas_call | solution.py:76
  710.3 1.0 copy-done.7
  711.4 0.2 fusion.3
  711.7 27.9 %exchange_zyxc_15.1 = f32[32,50,128]{2,1,0:T(8,128)S(1)} custom-call(f32[50,128]{1,0:T(8,128)S(1)} %reshape.111.src), custom_call_target="tpu_custom_call" | custom-call | tf_op jit(solution)/shard_map/exchange_zyxc_15/pallas_call | solution.py:76
  739.6 0.6 reshape.112
  740.6 1.3 copy.59
  742.0 0.5 convolution_bitcast_fusion
  742.4 0.5 copy.63
  742.9 0.6 reshape.123.src
  743.6 17.3 %exchange_zy_16.1 = f32[8,6,1760]{2,1,0:T(8,128)S(1)} custom-call(f32[8,6,1760]{2,1,0:T(8,128)S(1)} %reshape.123.src), custom_call_target="tpu_custom_call" | custom-call | tf_op jit(solution)/shard_map/exchange_zy_16/pallas_call | solution.py:76
  760.9 0.6 multiply_reduce_fusion.2
  761.6 0.6 broadcast_in_dim.9.src
  762.2 12.6 %exchange_zyxc_17.1 = f32[32,8,128]{2,1,0:T(8,128)S(1)} custom-call(f32[8,128]{1,0:T(8,128)S(1)} %broadcast_in_dim.9.src), custom_call_target="tpu_custom_call" | custom-call | tf_op jit(solution)/shard_map/exchange_zyxc_17/pallas_call | solution.py:76
  774.8 0.6 slice_reduce_fusion
  775.7 0.9 copy.60
  (31 shorter events, 1.4 us)
Async XLA Ops:
  447.4 4.0 copy-start.9
  463.7 2.5 copy-start
  504.1 1.7 copy-start.2
  505.8 3.1 copy-start.8
  527.9 1.8 copy-start.1
  567.8 1.1 copy-start.3
  586.2 1.1 copy-start.4
  606.8 1.0 copy-start.5
  710.2 1.1 copy-start.7
  740.5 1.4 copy-start.6

commit v3 on v0

v3 whole, which is shorter than its diff:
```python
import jax
import jax.numpy as jnp
from jax import lax
from jax.experimental import pallas as pl
from jax.experimental.pallas import tpu as pltpu
from jax.sharding import PartitionSpec as P

MESH = pl.DeviceIdType.MESH
F32 = jnp.float32
BF16 = jnp.bfloat16
SIZE = {"z": 4, "y": 2, "x": 2, "c": 2}
ALL = ("z", "y", "x", "c")
COUNT = 32
OTHERS = range(1, COUNT)
PLANE = ("c", "x", "y", "xc", "yc", "yx", "yxc")
LAG = 2
SLOTS = 8
BATCH = 16
TILE = 8
PAD = 48
EDGE = 3
NT = (((1,), (1,)), ((), ()))
TN = (((0,), (0,)), ((), ()))
LIMIT = 60 * 1024 * 1024


def place():
    a1 = lax.axis_index("a1")
    return {"z": lax.axis_index("a3"), "y": lax.axis_index("a2"), "x": a1 // 2, "c": lax.rem(a1, 2)}


def device(at):
    return (at["z"], at["y"], at["x"] * 2 + at["c"])


def block_of(at):
    return at["x"] * 2 + at["c"]


def member(at, group):
    index = 0
    for axis in group:
        index = index * SIZE[axis] + at[axis]
    return index


def flip(at, axes):
    return {axis: SIZE[axis] - 1 - at[axis] if axis in axes else at[axis] for axis in at}


def ahead(at, step):
    index = lax.rem(member(at, ALL) + step, COUNT)
    new = {}
    for axis in reversed(ALL):
        new[axis] = lax.rem(index, SIZE[axis])
        index = index // SIZE[axis]
    return new


def remote(src, dst, ss, rs, to):
    return pltpu.make_async_remote_copy(src_ref=src, dst_ref=dst, send_sem=ss, recv_sem=rs, device_id=device(to), device_id_type=MESH)


def greet(at):
    barrier = pltpu.get_barrier_semaphore()
    for step in OTHERS:
        pl.semaphore_signal(barrier, inc=1, device_id=device(ahead(at, step)), device_id_type=MESH)
    return barrier


def aligned(start, size):
    return pl.ds(pl.multiple_of(start, TILE), size)


def column_norm(power, axes):
    return jnp.sqrt(jnp.sum(power * power, axis=axes, keepdims=True))


def eights(shape, axis):
    return lax.broadcasted_iota(jnp.int32, shape, axis) // TILE


def in_eight(shape, axis):
    return lax.rem(lax.broadcasted_iota(jnp.int32, shape, axis), TILE)


def spread_blocks(rank, values, at, kron):
    blocks, _, width = kron.shape
    shape = (rank * TILE, rank)
    row = eights(shape, 0)
    sixth = rank // TILE
    quarter = row // sixth
    wanted = (lax.rem(quarter, 4) * 2 + quarter // 4) * sixth + lax.rem(row, sixth)
    picks = jnp.where(lax.broadcasted_iota(jnp.int32, shape, 1) == wanted, 1.0, 0.0).astype(BF16)
    spread = lax.dot_general(picks, values, NT, preferred_element_type=F32).astype(BF16)
    for block in range(blocks):
        shape = (values.shape[0], width)
        match = eights(shape, 1) + block * (width // TILE) == lax.broadcasted_iota(jnp.int32, shape, 0)
        wide = jnp.dot(spread, jnp.where(match, 1.0, 0.0).astype(BF16), preferred_element_type=F32)
        same = in_eight(wide.shape, 0) == in_eight(wide.shape, 1)
        kron[block] = jnp.where(same, wide, 0.0).astype(BF16)


def first_kernel(x_hbm, x_tiles, u3_ref, u2_ref, u1_ref, t_ref, x_all, new_ref, x_vmem, u3_rows, u2_rows, u1_rows, s_up, r_up, s_dn, r_dn,
                 own_tiles, y_part, y_recv, y_all, g_part, g_recv, p_send, p_all, free_up, free_dn, own_in, own_sem,
                 load_sem, ss_up, rs_up, ss_dn, rs_dn, x_send, x_recv,
                 y_ss, y_rs, c_ss, c_rs, w_ss, w_rs, f_ss, f_rs, g_ss, g_rs, p_ss, p_rs):
    frames, grid_w, grid_h = x_hbm.shape
    at = place()
    z, y = at["z"], at["y"]
    me = block_of(at)
    half = t_ref.shape[0] * TILE
    groups = x_all.shape[2]
    last = SIZE["z"] - 1
    edge = (z == 0) | (z == last)
    for part in range(frames // TILE):
        rows = pl.ds(part * TILE, TILE)
        pltpu.make_async_copy(x_hbm.at[rows], x_vmem.at[rows], load_sem.at[part]).start()
    barrier = greet(at)
    own = pltpu.make_async_copy(x_tiles.at[:, pl.ds(me * groups, groups)], own_tiles, own_in)
    own.start()
    for index in range(SIZE["z"]):
        @pl.when(z == index)
        def _():
            u3_rows[...] = u3_ref[:, index * grid_w:(index + 1) * grid_w].astype(BF16)

    for index in range(SIZE["y"]):
        @pl.when(y == index)
        def _():
            u2_rows[...] = u2_ref[:, index * grid_h:(index + 1) * grid_h].astype(BF16)

    for index in range(u1_rows.shape[0]):
        u1_rows[index] = u1_ref[:, index * frames:(index + 1) * frames].astype(BF16)

    @pl.when(jnp.logical_not(edge))
    def _():
        @pl.loop(0, frames)
        def _(frame):
            t_ref[:, frame] = jnp.zeros((half // TILE, TILE, grid_h), BF16)

    pl.semaphore_wait(barrier, COUNT - 1)

    core_pair, x_pair, y_pair = flip(at, "c"), flip(at, "x"), flip(at, "y")
    partners = [core_pair, x_pair, flip(at, "xc")]

    def swap_copy(way, frame):
        new = partners[way]
        return remote(x_tiles.at[frame, pl.ds(block_of(new) * groups, groups)], x_all.at[me, frame], x_send.at[way], x_recv.at[way], new)

    def link(slot, up):
        if up:
            return remote(s_up.at[slot], r_up.at[slot], ss_up.at[slot], rs_up.at[slot], {**at, "z": above})
        return remote(s_dn.at[slot], r_dn.at[slot], ss_dn.at[slot], rs_dn.at[slot], {**at, "z": below})

    def stream(frame, up):
        start, end, back, factor = (0, last, below, u3_rows[half:]) if up else (last, 0, above, u3_rows[:half])
        sends, recvs, free = (s_up, r_up, free_up) if up else (s_dn, r_dn, free_dn)

        @pl.when((frame >= 0) & (frame < frames))
        def _():
            slot = lax.rem(frame, SLOTS)
            copy = link(slot, up)
            part = jnp.dot(factor, x_vmem[frame], preferred_element_type=F32)

            @pl.when((z != end) & (frame >= SLOTS))
            def _():
                copy.wait_send()
                pl.semaphore_wait(free, 1)

            sends[slot] = part

            @pl.when(z != start)
            def _():
                copy.wait_recv()
                sends[slot] += recvs[slot]

                @pl.when(frame + SLOTS < frames)
                def _():
                    pl.semaphore_signal(free, inc=1, device_id=device({**at, "z": back}), device_id_type=MESH)

            @pl.when(z != end)
            def _():
                copy.start()

            @pl.when(z == end)
            def _():
                done = sends[slot].astype(BF16)
                t_ref[:, frame] = done.reshape(half // TILE, TILE, grid_h)
                rows = lax.dot_general(done, u2_rows[...], NT, preferred_element_type=F32)
                y_part[:, pl.ds(frame, 1), :] = rows[:, None, :]

    side = half // 2
    keep, give = pl.ds(y * side, side), pl.ds((1 - y) * side, side)

    def rows_at(batch):
        return pl.ds(pl.multiple_of(batch * BATCH, BATCH), BATCH)

    def y_copy(batch):
        rows = rows_at(batch)
        return remote(y_part.at[give, rows, :], y_recv.at[:, rows, :], y_ss.at[batch], y_rs.at[batch], y_pair)

    def spread_copy(owner, batch, pair, ss, rs):
        block = y_all.at[owner, :, rows_at(batch), :]
        return remote(block, block, ss.at[batch], rs.at[batch], pair)

    far = block_of(x_pair)

    def settle(batch):
        y_copy(batch).wait_recv()
        rows = rows_at(batch)
        y_all[me, :, rows, :] = (y_part[keep, rows, :] + y_recv[:, rows, :]).astype(BF16)
        spread_copy(me, batch, core_pair, c_ss, c_rs).start()
        spread_copy(me, batch, x_pair, w_ss, w_rs).start()

    def forward(batch):
        spread_copy(me, batch, x_pair, w_ss, w_rs).wait_recv()
        spread_copy(far, batch, core_pair, f_ss, f_rs).start()

    own.wait()
    put = pltpu.make_async_copy(own_tiles, x_all.at[me], own_sem)
    put.start()
    above = jnp.minimum(z + 1, last)
    below = jnp.maximum(z - 1, 0)
    lead = jnp.minimum(z, last - z)

    @pl.loop(0, frames + last * LAG)
    def _(step):
        newest = step - LAG * lead

        @pl.when(step < frames)
        def _():
            for way in range(len(partners)):
                swap_copy(way, jnp.minimum(step, frames - 1)).start()

        @pl.when((newest >= 0) & (newest < frames) & (lax.rem(newest, TILE) == 0))
        def _():
            part = newest // TILE
            rows = aligned(part * TILE, TILE)
            pltpu.make_async_copy(x_hbm.at[rows], x_vmem.at[rows], load_sem.at[part]).wait()

        stream(step - LAG * z, True)
        stream(step - LAG * (last - z), False)
        final = step - last * LAG

        @pl.when(edge & (final >= 0))
        def _():
            place_in = lax.rem(final, BATCH)
            batch = final // BATCH

            @pl.when(place_in == BATCH - 1)
            def _():
                y_copy(batch).start()

            @pl.when((place_in == BATCH // 2) & (batch >= 1))
            def _():
                settle(batch - 1)

            @pl.when((place_in == BATCH // 2) & (batch >= 3))
            def _():
                forward(batch - 3)

    batches = frames // BATCH
    piece = frames // 4
    quads = [flip(at, axes) for axes in ("y", "z", "yz")]

    def quad_rows(to):
        return aligned((to["z"] // EDGE * 2 + to["y"]) * piece, piece)

    def g_copy(way):
        return remote(g_part.at[:, quad_rows(quads[way]), :], g_recv.at[way], g_ss.at[way], g_rs.at[way], quads[way])

    slot16 = (me * 2 + z // EDGE) * 2 + y

    def p_copy(step):
        return remote(p_send, p_all.at[slot16], p_ss.at[step - 1], p_rs.at[slot16], ahead(at, step))

    @pl.when(edge)
    def _():
        settle(batches - 1)
        for batch in range(batches - 3, batches):
            forward(batch)
        for batch in range(batches):
            spread_copy(me, batch, core_pair, c_ss, c_rs).wait_recv()
            spread_copy(far, batch, core_pair, f_ss, f_rs).wait_recv()
        g_part[...] = jnp.zeros(g_part.shape, F32)

        @pl.loop(0, side)
        def _(col):
            left = y_all[me, col]
            for r in range(g_part.shape[0]):
                g_part[r] += lax.dot_general(left, y_all[r, col], NT, preferred_element_type=F32)

        for way in range(len(quads)):
            g_copy(way).start()
        for way in range(len(quads)):
            g_copy(way).wait_recv()
        power = jnp.zeros(p_send.shape, F32)
        for r in range(g_part.shape[0]):
            gram = g_part[r, quad_rows(at), :]
            for way in range(len(quads)):
                gram = gram + g_recv[way, r]
            power = power + lax.dot_general(gram.astype(BF16), u1_rows[r], NT, preferred_element_type=F32)
        p_send[...] = power
        p_all[slot16] = power
        for step in OTHERS:
            p_copy(step).start()
        for way in range(len(quads)):
            g_copy(way).wait_send()
        for batch in range(batches):
            y_copy(batch).wait_send()
            spread_copy(me, batch, core_pair, c_ss, c_rs).wait_send()
            spread_copy(me, batch, x_pair, w_ss, w_rs).wait_send()
            spread_copy(far, batch, core_pair, f_ss, f_rs).wait_send()

    for source in range(p_all.shape[0]):
        @pl.when(jnp.logical_not(edge) | (slot16 != source))
        def _():
            remote(p_send, p_all.at[source], p_ss.at[0], p_rs.at[source], ahead(at, 1)).wait_recv()

    new_ref[...] = p_all[...] / column_norm(p_all[...], (0, 1))

    @pl.when(edge)
    def _():
        for step in OTHERS:
            p_copy(step).wait_send()

    for slot in range(SLOTS):
        @pl.when(z < last)
        def _():
            link(slot, True).wait_send()

        @pl.when(z > 0)
        def _():
            link(slot, False).wait_send()

    put.wait()
    for way in range(len(partners)):
        swap_copy(way, pl.ds(0, frames)).wait()


def dma(*shape):
    return pltpu.SemaphoreType.DMA(shape)


def first_stage(tensor_t, u3_t, u2_t, u1_t):
    frames, grid_w, grid_h = tensor_t.shape
    half, rank_h, rank_t = u3_t.shape[0] // 2, u2_t.shape[0], u1_t.shape[0]
    link = pltpu.VMEM((SLOTS, half, grid_h), F32)
    any_space = pl.BlockSpec(memory_space=pl.ANY)
    vmem = pl.BlockSpec(memory_space=pltpu.VMEM)
    piece = frames // 4
    groups = grid_w // (4 * TILE)
    return pl.pallas_call(
        first_kernel,
        out_shape=(jax.ShapeDtypeStruct((half // TILE, frames, TILE, grid_h), BF16),
                   jax.ShapeDtypeStruct((4, frames, groups, TILE, grid_h), BF16),
                   jax.ShapeDtypeStruct((16, piece, rank_t), F32)),
        in_specs=[any_space, any_space, vmem, vmem, vmem],
        out_specs=(vmem, any_space, vmem),
        scratch_shapes=[pltpu.VMEM(tensor_t.shape, BF16), pltpu.VMEM((u3_t.shape[0], grid_w), BF16),
                        pltpu.VMEM((rank_h, grid_h), BF16), pltpu.VMEM((4, rank_t, frames), BF16), link, link, link, link,
                        pltpu.VMEM((frames, groups, TILE, grid_h), BF16),
                        pltpu.VMEM((half, frames, rank_h), F32), pltpu.VMEM((half // 2, frames, rank_h), F32),
                        pltpu.VMEM((4, half // 2, frames, rank_h), BF16),
                        pltpu.VMEM((4, frames, frames), F32), pltpu.VMEM((3, 4, piece, frames), F32),
                        pltpu.VMEM((piece, rank_t), F32), pltpu.VMEM((16, piece, rank_t), F32),
                        pltpu.SemaphoreType.REGULAR, pltpu.SemaphoreType.REGULAR, pltpu.SemaphoreType.DMA, pltpu.SemaphoreType.DMA,
                        dma(frames // TILE)] + [dma(SLOTS)] * 4 + [dma(3)] * 2 + [dma(frames // BATCH)] * 8 + [dma(3)] * 2
                       + [dma(COUNT), dma(16)],
        compiler_params=pltpu.CompilerParams(collective_id=1, has_side_effects=True, vmem_limit_bytes=LIMIT),
        name="first_stage",
    )(tensor_t, tensor_t.reshape(frames, grid_w // TILE, TILE, grid_h), u3_t, u2_t, u1_t)


def height_part(at, x_hbm, t_ref, u1_ref, u2_ref, z_out, height_ref, x_slots, kron, y_part, y_core, y_x, y_own, y_other,
                g_part, g_core, g_recv, z_send, p_send, p_all, k_ss, k_rs,
                load_sem, c_ss, c_rs, w_ss, w_rs, y_ss, y_rs, z_ss, z_rs, g_ss, g_rs, p_ss, p_rs):
    barrier = greet(at)
    z, y, x, c = at["z"], at["y"], at["x"], at["c"]
    me = block_of(at)
    edge = (z == 0) | (z == SIZE["z"] - 1)
    blocks, frames, groups, _, grid_h = x_hbm.shape
    rank = u1_ref.shape[1]
    slots = x_slots.shape[0]
    core_pair, x_pair, y_pair = flip(at, "c"), flip(at, "x"), flip(at, "y")

    def load(group):
        slot = lax.rem(group, slots)
        return pltpu.make_async_copy(x_hbm.at[:, :, group], x_slots.at[slot], load_sem.at[slot])

    for group in range(slots):
        load(group).start()
    spread_blocks(rank, u1_ref[...].astype(BF16), at, kron)
    g_part[...] = jnp.zeros(g_part.shape, F32)
    pl.semaphore_wait(barrier, COUNT - 1)

    half, quart = rank // 2, rank // 4

    def core_copy(g):
        return remote(y_part.at[g, pl.ds((1 - c) * half, half)], y_core.at[g], c_ss.at[g], c_rs.at[g], core_pair)

    def wide_copy(g):
        return remote(y_core.at[g, pl.ds((1 - x) * quart, quart)], y_x.at[g], w_ss.at[g], w_rs.at[g], x_pair)

    def tall_copy(g):
        return remote(y_own.at[g], y_other.at[g], y_ss.at[g], y_rs.at[g], y_pair)

    def z_copy(g):
        return remote(z_send.at[g], z_out.at[y, g], z_ss.at[g], z_rs.at[g], y_pair)

    def widen(g):
        core_copy(g).wait_recv()
        y_core[g] += y_part[g, pl.ds(c * half, half)]
        wide_copy(g).start()

    @pl.when(edge)
    def _():
        @pl.loop(0, groups)
        def _(g):
            part = jnp.dot(kron[me], t_ref[g].reshape(frames * TILE, grid_h), preferred_element_type=F32)
            y_part[g] = part.reshape(rank, TILE, grid_h)
            core_copy(g).start()

            @pl.when(g >= 2)
            def _():
                widen(g - 2)

        widen(groups - 2)
        widen(groups - 1)

    def gram(g):
        tall_copy(g).wait_recv()
        left = y_own[g].reshape(quart * TILE, grid_h)
        right = y_other[g].reshape(quart * TILE, grid_h)
        rows = slice(0, grid_h)
        g_part[y, rows, :] += lax.dot_general(left, left, TN, preferred_element_type=F32)
        g_part[1 - y, rows, :] += lax.dot_general(left, right, TN, preferred_element_type=F32)

    @pl.loop(0, groups)
    def _(g):
        load(g).wait()
        slot = lax.rem(g, slots)
        acc = jnp.zeros((rank * TILE, grid_h), F32)
        for block in range(blocks):
            acc = acc + jnp.dot(kron[block], x_slots[slot, block].reshape(frames * TILE, grid_h), preferred_element_type=F32)

        @pl.when(g + slots < groups)
        def _():
            load(g + slots).start()

        whole = acc.reshape(2, half, TILE, grid_h).astype(BF16)
        for index in range(SIZE["y"]):
            @pl.when(y == index)
            def _():
                z_out[index, g] = whole[index]
                z_send[g] = whole[1 - index]

        @pl.when(edge)
        def _():
            wide_copy(g).wait_recv()
            y_own[g] = (y_core[g, pl.ds(x * quart, quart)] + y_x[g]).astype(BF16)
            tall_copy(g).start()

            @pl.when(g >= 2)
            def _():
                gram(g - 2)

        @pl.when(lax.rem(g, 2) == 1)
        def _():
            z_copy(g // 2).start()

    @pl.loop(groups // 2, groups)
    def _(g):
        z_copy(g).start()

    core_rows = g_part.shape[1] // 2
    piece = core_rows // 4
    quads = [flip(at, axes) for axes in ("x", "z", "xz")]

    def k_copy():
        return remote(g_part.at[:, aligned((1 - c) * core_rows, core_rows), :], g_core, k_ss, k_rs, core_pair)

    def quad_rows(to):
        return aligned(c * core_rows + (to["x"] * 2 + to["z"] // EDGE) * piece, piece)

    def g_copy(way):
        return remote(g_part.at[:, quad_rows(quads[way]), :], g_recv.at[way], g_ss.at[way], g_rs.at[way], quads[way])

    slot16 = ((y * 2 + c) * 2 + x) * 2 + z // EDGE

    def p_copy(step):
        return remote(p_send, p_all.at[slot16], p_ss.at[step - 1], p_rs.at[slot16], ahead(at, step))

    @pl.when(edge)
    def _():
        gram(groups - 2)
        gram(groups - 1)
        k_copy().start()
        k_copy().wait_recv()
        g_part[:, aligned(c * core_rows, core_rows), :] += g_core[...]
        for way in range(len(quads)):
            g_copy(way).start()
        for way in range(len(quads)):
            g_copy(way).wait_recv()
        power = jnp.zeros(p_send.shape, F32)
        for r in range(g_part.shape[0]):
            full = g_part[r, quad_rows(at), :]
            for way in range(len(quads)):
                full = full + g_recv[way, r]
            power = power + jnp.dot(full.astype(BF16), u2_ref[r], preferred_element_type=F32)
        p_send[...] = power
        p_all[slot16] = power
        for step in OTHERS:
            p_copy(step).start()
        k_copy().wait_send()
        for way in range(len(quads)):
            g_copy(way).wait_send()

        @pl.loop(0, groups)
        def _(g):
            core_copy(g).wait_send()
            wide_copy(g).wait_send()
            tall_copy(g).wait_send()

    for source in range(p_all.shape[0]):
        @pl.when(jnp.logical_not(edge) | (slot16 != source))
        def _():
            remote(p_send, p_all.at[source], p_ss.at[0], p_rs.at[source], ahead(at, 1)).wait_recv()

    height_ref[...] = p_all[...] / column_norm(p_all[...], (0, 1))

    @pl.when(edge)
    def _():
        for step in OTHERS:
            p_copy(step).wait_send()

    @pl.loop(0, groups)
    def _(g):
        z_copy(g).wait()


def width_part(at, z_ref, height_ref, u3_ref, new_ref, core_ref, energy_ref, u2_cols, y_send, y_recv, y_own, y_line, g_part, g_core, g_quad,
               p_all, q_send, q_all, c_send, c_recv, e_send, e_all,
               a_ss, a_rs, r_ss, l_ss, b_rs, k_ss, k_rs, d_ss, d_rs, q_ss, q_rs, p_ss, p_rs, f_ss, f_rs, n_ss, n_rs, e_ss, e_rs, h_ss, h_rs):
    z, y, x, c = at["z"], at["y"], at["x"], at["c"]
    me = block_of(at)
    mine = member(at, ALL)
    last = SIZE["z"] - 1
    sources, groups, many, eight, grid_h = z_ref.shape
    width = groups * eight
    six = many // 4
    span = 4 * width
    rank_h = height_ref.shape[2]
    side_h = rank_h // 2
    u2_cols[...] = jnp.zeros(u2_cols.shape, BF16)
    for s in range(sources):
        half = height_ref.shape[0] // 2
        rows = height_ref[s * half:(s + 1) * half].reshape(half * height_ref.shape[1], rank_h)[:grid_h]
        cols = rows.T.astype(BF16)
        for side in range(2):
            u2_cols[s, side * PAD:side * PAD + side_h, :] = cols[side * side_h:(side + 1) * side_h]
    for a in range(many):
        acc = jnp.zeros((2 * PAD, width), F32)
        for s in range(sources):
            acc = acc + lax.dot_general(u2_cols[s], z_ref[s, :, a].reshape(width, grid_h), NT, preferred_element_type=F32)
        for side in range(2):
            y_send[a // six, side, (a % six) * PAD:(a % six + 1) * PAD, :] = acc[side * PAD:(side + 1) * PAD].astype(BF16)
    y_recv[me] = y_send[me]
    mates = [flip(at, axes) for axes in ("x", "xc", "c")]

    def quarter_copy(way):
        return remote(y_send.at[block_of(mates[way])], y_recv.at[me], a_ss.at[way], a_rs.at[way], mates[way])

    for way in range(len(mates)):
        quarter_copy(way).start()
    for way in range(len(mates)):
        quarter_copy(way).wait_recv()
    sides = []
    for side in range(2):
        whole = jnp.concatenate([y_recv[q, side].astype(F32) for q in range(4)], axis=1)
        y_own[side] = whole.astype(BF16)
        sides.append(whole)
    y_line[z] = jnp.concatenate(sides, axis=1).astype(BF16)

    right = {**at, "z": jnp.minimum(z + 1, last)}
    left = {**at, "z": jnp.maximum(z - 1, 0)}

    def line_copy(block, to, ss):
        return remote(y_line.at[block], y_line.at[block], ss.at[block], b_rs.at[block], to)

    def pick(values):
        value = values[-1]
        for index in range(last):
            value = jnp.where(z == index, values[index], value)
        return value

    order = [z, pick((1, 0, 1, 2)), pick((2, 2, 3, 1)), pick((3, 3, 0, 0))]
    half_rows = span // 2
    piece = half_rows // 4
    core_pair = flip(at, "c")
    plane = [flip(at, axes) for axes in PLANE]
    quads = [flip(at, axes) for axes in ("x", "y", "yx")]
    ways = range(len(quads))

    def k_copy(block):
        return remote(g_part.at[block, aligned((1 - c) * half_rows, half_rows), :], g_core.at[block], k_ss.at[block], k_rs.at[block], core_pair)

    def quad_rows(to):
        return aligned(c * half_rows + (to["x"] * 2 + to["y"]) * piece, piece)

    def d_copy(block, way):
        return remote(g_part.at[block, quad_rows(quads[way]), :], g_quad.at[way, block], d_ss.at[way, block], d_rs.at[way, block], quads[way])

    def gram(block):
        acc = jnp.zeros((span, span), F32)
        for side in range(2):
            wide = lax.dot_general(y_own[side], y_line[block], TN, preferred_element_type=F32)
            acc = acc + wide[:, side * span:(side + 1) * span]
        g_part[block] = acc
        k_copy(block).start()

    def settle(block):
        k_copy(block).wait_recv()
        g_part[block, aligned(c * half_rows, half_rows), :] += g_core[block]
        for way in ways:
            d_copy(block, way).start()

    def power_of(block):
        full = g_part[block, quad_rows(at), :]
        for way in ways:
            d_copy(block, way).wait_recv()
            full = full + g_quad[way, block]
        return jnp.dot(full.astype(BF16), u3_ref[block], preferred_element_type=F32)

    def pass_on(block):
        @pl.when((block <= z) & (z < last))
        def _():
            line_copy(block, right, r_ss).start()

        @pl.when((block >= z) & (z > 0))
        def _():
            line_copy(block, left, l_ss).start()

    pass_on(z)
    power = jnp.zeros((piece, p_all.shape[3]), F32)
    for k in range(len(order) + 2):
        if k < len(order):
            if k > 0:
                line_copy(order[k], right, r_ss).wait_recv()
                pass_on(order[k])
            gram(order[k])
        if 1 <= k <= len(order):
            settle(order[k - 1])
        if k >= 2:
            power = power + power_of(order[k - 2])

    slot = (c * 2 + x) * 2 + y
    p_all[z, slot] = power
    q_send[...] = jnp.broadcast_to(jnp.sum(power * power, axis=0, keepdims=True), q_send.shape)
    q_all[mine] = q_send[...]

    def q_copy(step):
        return remote(q_send, q_all.at[mine], q_ss.at[step - 1], q_rs.at[COUNT - step - 1], ahead(at, step))

    def rows_copy(owner, ss, rs, to):
        block = p_all.at[owner, slot]
        return remote(block, block, ss, rs, to)

    def p_copy(way):
        return rows_copy(z, p_ss.at[way], p_rs.at[way], plane[way])

    def behind(hop):
        return lax.rem(z + SIZE["z"] - hop, SIZE["z"])

    def n_copy(hop, owner):
        return rows_copy(owner, n_ss.at[hop - 1], n_rs.at[hop - 1], {**at, "z": lax.rem(z + hop, SIZE["z"])})

    def f_copy(way, hop):
        return rows_copy(behind(hop), f_ss.at[way, hop - 1], f_rs.at[way, hop - 1], plane[way])

    hops = range(1, SIZE["z"])
    paths = range(len(plane))
    for step in OTHERS:
        q_copy(step).start()
    for way in paths:
        p_copy(way).start()
    for hop in hops:
        n_copy(hop, z).start()
    for way in paths:
        p_copy(way).wait_recv()
    for step in OTHERS:
        q_copy(step).wait_recv()
    norm = jnp.sqrt(jnp.sum(q_all[:, 0, :], axis=0, keepdims=True))
    factor = (p_all[z].reshape(span, p_all.shape[3]) / norm).astype(BF16)
    fourth = p_all.shape[3] // 4
    for side in range(2):
        part = lax.dot_general(factor, y_own[side], (((0,), (1,)), ((), ())), preferred_element_type=F32)
        for to in range(4):
            c_send[to, side] = part[to * fourth:(to + 1) * fourth]

    zy = z * 2 + y
    c_recv[zy] = c_send[z, y]
    spots = c_recv.shape[0]

    def c_copy(step):
        index = lax.rem(zy + step, spots)
        new = {**at, "z": index // 2, "y": lax.rem(index, 2)}
        return remote(c_send.at[new["z"], new["y"]], c_recv.at[zy], h_ss.at[step - 1], h_rs.at[step - 1], new)

    for step in range(1, spots):
        c_copy(step).start()
    for hop in hops:
        n_copy(hop, behind(hop)).wait_recv()
        for way in paths:
            f_copy(way, hop).start()
    for step in range(1, spots):
        c_copy(step).wait_recv()
    squares = jnp.zeros((1, c_recv.shape[2]), F32)
    for side in range(2):
        full = c_recv[side]
        for source in range(side + 2, spots, 2):
            full = full + c_recv[source]
        core_ref[side] = full
        squares = squares + jnp.sum(full * full, axis=0, keepdims=True)
    e_send[...] = jnp.broadcast_to(jnp.sum(squares, axis=1, keepdims=True), e_send.shape)
    e_all[mine] = e_send[...]

    def e_copy(step):
        return remote(e_send, e_all.at[mine], e_ss.at[step - 1], e_rs.at[COUNT - step - 1], ahead(at, step))

    for step in OTHERS:
        e_copy(step).start()
    for hop in hops:
        for way in paths:
            f_copy(way, hop).wait_recv()
    new_ref[...] = p_all[...] / norm[None, None]
    for step in OTHERS:
        e_copy(step).wait_recv()
    energy_ref[...] = jnp.sum(e_all[...], axis=0)

    for way in range(len(mates)):
        quarter_copy(way).wait_send()
    for block in order:
        @pl.when((block <= z) & (z < last))
        def _():
            line_copy(block, right, r_ss).wait_send()

        @pl.when((block >= z) & (z > 0))
        def _():
            line_copy(block, left, l_ss).wait_send()

        k_copy(block).wait_send()
        for way in ways:
            d_copy(block, way).wait_send()
    for step in OTHERS:
        q_copy(step).wait_send()
        e_copy(step).wait_send()
    for way in paths:
        p_copy(way).wait_send()
        for hop in hops:
            f_copy(way, hop).wait_send()
    for hop in hops:
        n_copy(hop, z).wait_send()
    for step in range(1, spots):
        c_copy(step).wait_send()


HEIGHT_SCRATCH = 28


def second_kernel(x_hbm, t_ref, u1_ref, u2_ref, u3_ref, height_ref, new_ref, core_ref, energy_ref, z_all, *scratch):
    at = place()
    height_part(at, x_hbm, t_ref, u1_ref, u2_ref, z_all, height_ref, *scratch[:HEIGHT_SCRATCH])
    width_part(at, z_all, height_ref, u3_ref, new_ref, core_ref, energy_ref, *scratch[HEIGHT_SCRATCH:])


def second_stage(x_all, t_mat, new_time, u2, u3):
    blocks, frames, groups, _, grid_h = x_all.shape
    rank, rank_h, rank_w = new_time.shape[1], u2.shape[1], u3.shape[1]
    vmem = pl.BlockSpec(memory_space=pltpu.VMEM)
    rows = 384
    piece = rows // TILE
    width = groups * TILE
    cols = rank // TILE * PAD
    small = width // 2
    fourth = rank_w // 4

    def f32(*shape):
        return pltpu.VMEM(shape, F32)

    def bf16(*shape):
        return pltpu.VMEM(shape, BF16)

    one = pltpu.SemaphoreType.DMA
    height = [bf16(4, blocks, frames, TILE, grid_h), bf16(blocks, rank * TILE, frames * TILE),
              f32(groups, rank, TILE, grid_h), f32(groups, rank // 2, TILE, grid_h), f32(groups, rank // 4, TILE, grid_h),
              bf16(groups, rank // 4, TILE, grid_h), bf16(groups, rank // 4, TILE, grid_h),
              f32(2, rows, grid_h), f32(2, rows // 2, grid_h), f32(3, 2, piece, grid_h),
              bf16(groups, rank // 2, TILE, grid_h), f32(piece, rank_h), f32(16, piece, rank_h), one, one,
              dma(4)] + [dma(groups)] * 8 + [dma(3), dma(3), dma(COUNT), dma(16)]
    wide = [bf16(2, 2 * PAD, grid_h), bf16(4, 2, cols, width), bf16(4, 2, cols, width), bf16(2, cols, 4 * width), bf16(4, cols, 2 * 4 * width),
            f32(4, 4 * width, 4 * width), f32(4, 2 * width, 4 * width), f32(3, 4, small, 4 * width),
            f32(4, 2 * 4, small, rank_w), f32(TILE, rank_w), f32(COUNT, TILE, rank_w),
            f32(4, 2, fourth, cols), f32(2 * 4, fourth, cols), f32(TILE, 128), f32(COUNT, TILE, 128),
            dma(3), dma(3)] + [dma(4)] * 5 + [dma(3, 4), dma(3, 4), dma(COUNT), dma(COUNT)] + [dma(7)] * 2 + [dma(7, 3)] * 2 + [dma(3)] * 2 \
        + [dma(COUNT)] * 2 + [dma(7)] * 2
    return pl.pallas_call(
        second_kernel,
        out_shape=(jax.ShapeDtypeStruct((16, piece, rank_h), F32),
                   jax.ShapeDtypeStruct((4, 2 * 4, small, rank_w), F32),
                   jax.ShapeDtypeStruct((2, fourth, cols), F32),
                   jax.ShapeDtypeStruct((TILE, 128), F32)),
        in_specs=[pl.BlockSpec(memory_space=pl.ANY), vmem, vmem, vmem, vmem],
        out_specs=(vmem, vmem, vmem, vmem),
        scratch_shapes=[bf16(2, groups, rank // 2, TILE, grid_h)] + height + wide,
        compiler_params=pltpu.CompilerParams(collective_id=2, has_side_effects=True, vmem_limit_bytes=LIMIT),
        name="second_stage",
    )(x_all, t_mat, new_time, u2.astype(BF16).reshape(2, grid_h, rank_h), u3.astype(BF16).reshape(4, 4 * width, rank_w))


def solution(mesh):
    def local_sweep(tensor, u_time, u_height, u_width):
        frames, grid_h, grid_w = tensor.shape
        rank_t, rank_h, rank_w = u_time.shape[1], u_height.shape[1], u_width.shape[1]
        t_mat, x_all, new_time = first_stage(tensor.swapaxes(1, 2), u_width.T, u_height.T, u_time.T)
        new_time = new_time.reshape(-1, rank_t)
        power, new_width, core, energy = second_stage(x_all, t_mat, new_time, u_height, u_width)
        new_height = power.reshape(2, -1, rank_h)[:, :grid_h].reshape(-1, rank_h)
        new_width = new_width.reshape(-1, rank_w)
        core = core.reshape(2, rank_w // 4, rank_t // 8, PAD)[..., :rank_h // 2].transpose(0, 2, 3, 1)
        core_tensor = core.reshape(rank_t // 4, rank_h // 2, rank_w // 4)
        return new_time, new_height, new_width, core_tensor, energy[0, 0]

    return jax.shard_map(local_sweep, mesh=mesh, in_specs=(P("a1", "a2", "a3"), P(), P(), P()), out_specs=(P(), P(), P(), P("a1", "a2", "a3"), P()), check_vma=False)
```

time: 1460 us -> 485 us (0.33)
  blocking collectives: 625 us -> 0 us
  waiting for transfers between devices: 486 us -> 0 us
  Pallas kernels: 0 us -> 472 us
  local copies, waits for them, and re-layouts: 264 us -> 10.1 us
  matrix products: 50.6 us -> 0 us
  between operations: 15.6 us -> 0.69 us
    pallas_call x0 -> x2, Pallas kernels: none -> 472 us  [the longest x1 315 us: first_stage(): pl.pallas_call(first_kernel, out_shape=(jax.ShapeDtypeStruct((half // TIL...]
    reduce_scatter x4 -> x0, waiting for transfers between devices: 446 us -> none  [the longest x1 391 us: local_sweep(): lax.psum_scatter(t_part.reshape(frames, grid_h, -1), 'a3', scatter_dimens...]
    psum x7 -> x0, blocking collectives: 294 us -> none  [the longest x3 233 us: gram_update(): gram_rows = lax.psum(gram_part, sum_axes).astype(jnp.bfloat16)]
    unnamed x2 -> x0, blocking collectives: 292 us -> none
    unnamed x21 -> x4, local copies, waits for them, and re-layouts: 137 us -> 3.33 us
    reshape x9 -> x2, local copies, waits for them, and re-layouts: 113 us -> 1.9 us  [the longest x1 1.04 us: local_sweep(): core.reshape(2, rank_w // 4, rank_t // 8, PAD)[..., :rank_h // 2]]
    dot_general x12 -> x0, matrix products: 50.6 us -> none  [the longest x1 14.7 us: local_sweep(): jnp.dot(tensor.reshape(frames * grid_h, grid_w), rows_of(u_width, 'a3', g...]
    all_gather x2 -> x0, waiting for transfers between devices: 39.7 us -> none  [gram_update(): all_rows = lax.all_gather(local_rows, row_axes, axis=0, tiled=True)]
  transfers between devices with their start and end apart: 7 -> 0, of which waited for: 4 -> 0; matrix products, arithmetic and copies ran while one was open for 9% -> 0% of each run, Pallas kernels for 0% -> 0%
where the time goes in v3:
time: 485 us
  Pallas kernels  472 us (97%)
  local copies, waits for them, and re-layouts  10.1 us (2%)
    pallas_call x1, Pallas kernels, first_stage(): pl.pallas_call(first_kernel, out_shape=(jax.ShapeDtypeStruct((half // TIL...  315 us
    pallas_call x1, Pallas kernels, second_stage(): pl.pallas_call(second_kernel, out_shape=(jax.ShapeDtypeStruct((16, piece,...  157 us

profile of v3, /device:TPU:0, one launch (start us, length us, event | category | flops | bytes accessed | tf_op | source)
XLA Modules:
  0.0 485.0 jit_solution(9393268975634274008)
XLA Ops:
  0.6 1.0 convert_element_type.6
  1.6 0.8 copy.20
  2.4 1.2 convert_element_type.7
  3.6 1.1 copy.21
  4.7 314.9 %first_stage.1 = (bf16[10,96,8,360]{3,2,1,0:T(8,128)(2,1)}, bf16[4,96,10,8,360]{4,3,2,1,0:T(8,128)(2,1)}, f32[16,24,48]{2,1,0:T(8,128)}) custom-call(bf16[96,320,360]{2,1,0:T(8,128)(2,1)} %bitcast.16, bf16[96,40,8,360]{3,2,1,0:T(8,128)(2,1)} %bitcast.17, f32[160,1280]{1,0:T(8,128)} %bitcast.18, f32[88,720]{1,0:T(8,128)} %bitcast.22, f32[48,384]{1,0:T(8,128)} %bitcast.28), custom_call_target="tpu_custom_call" | custom-call | tf_op jit(solution)/shard_map/first_stage/pallas_call | solution.py:353
  319.6 0.0 copy-start
  319.6 157.2 %second_stage.1 = (f32[16,48,88]{2,1,0:T(8,128)}, f32[4,8,40,160]{3,2,1,0:T(8,128)}, f32[2,40,288]{2,1,0:T(8,128)}, f32[8,128]{1,0:T(8,128)}) custom-call(bf16[4,96,10,8,360]{4,3,2,1,0:T(8,128)(2,1)} %get-tuple-element.13.x_hbm, bf16[10,96,8,360]{3,2,1,0:T(8,128)(2,1)} %get-tuple-element.14.t_ref, f32[384,48]{1,0:T(8,128)} %bitcast.23, ...), custom_call_target="tpu_custom_call" | custom-call | tf_op jit(solution)/shard_map/second_stage/pallas_call | solution.py:807
  476.8 0.0 copy-done
  476.8 0.7 copy.24
  477.5 1.2 slice.11
  478.7 1.0 slice.12
  479.7 0.9 copy.26
  480.6 2.6 copy.25
  483.2 1.0 reshape.44
  484.2 0.7 copy.23
  (1 shorter events, 0.0 us)
Async XLA Ops:
  319.6 157.2 %copy-start = (f32[16,24,48]{2,1,0:T(8,128)S(1)}, f32[16,24,48]{2,1,0:T(8,128)}, u32[]{:S(2)}) copy-start(f32[16,24,48]{2,1,0:T(8,128)} %get-tuple-element.12) | copy-start | bytes 221188

commit v4 on v3

--- a/solution.py
+++ b/solution.py
@@ -129,8 +129,7 @@
         def _():
             u2_rows[...] = u2_ref[:, index * grid_h:(index + 1) * grid_h].astype(BF16)
 
-    for index in range(u1_rows.shape[0]):
-        u1_rows[index] = u1_ref[:, index * frames:(index + 1) * frames].astype(BF16)
+    u1_rows[...] = u1_ref[...].astype(BF16)
 
     @pl.when(jnp.logical_not(edge))
     def _():
@@ -267,7 +266,7 @@
         return aligned((to["z"] // EDGE * 2 + to["y"]) * piece, piece)
 
     def g_copy(way):
-        return remote(g_part.at[:, quad_rows(quads[way]), :], g_recv.at[way], g_ss.at[way], g_rs.at[way], quads[way])
+        return remote(g_part.at[quad_rows(quads[way]), :], g_recv.at[way], g_ss.at[way], g_rs.at[way], quads[way])
 
     slot16 = (me * 2 + z // EDGE) * 2 + y
 
@@ -284,22 +283,23 @@
             spread_copy(far, batch, core_pair, f_ss, f_rs).wait_recv()
         g_part[...] = jnp.zeros(g_part.shape, F32)
 
-        @pl.loop(0, side)
-        def _(col):
-            left = y_all[me, col]
-            for r in range(g_part.shape[0]):
-                g_part[r] += lax.dot_general(left, y_all[r, col], NT, preferred_element_type=F32)
+        @pl.loop(0, side // 4)
+        def _(four):
+            acc = g_part[...]
+            for step in range(4):
+                col = four * 4 + step
+                right = y_all[:, col].reshape(y_all.shape[0] * frames, y_all.shape[3])
+                acc = acc + lax.dot_general(y_all[me, col], right, NT, preferred_element_type=F32)
+            g_part[...] = acc
 
         for way in range(len(quads)):
             g_copy(way).start()
         for way in range(len(quads)):
             g_copy(way).wait_recv()
-        power = jnp.zeros(p_send.shape, F32)
-        for r in range(g_part.shape[0]):
-            gram = g_part[r, quad_rows(at), :]
-            for way in range(len(quads)):
-                gram = gram + g_recv[way, r]
-            power = power + lax.dot_general(gram.astype(BF16), u1_rows[r], NT, preferred_element_type=F32)
+        gram = g_part[quad_rows(at), :]
+        for way in range(len(quads)):
+            gram = gram + g_recv[way]
+        power = lax.dot_general(gram.astype(BF16), u1_rows[...], NT, preferred_element_type=F32)
         p_send[...] = power
         p_all[slot16] = power
         for step in OTHERS:
@@ -358,11 +358,11 @@
         in_specs=[any_space, any_space, vmem, vmem, vmem],
         out_specs=(vmem, any_space, vmem),
         scratch_shapes=[pltpu.VMEM(tensor_t.shape, BF16), pltpu.VMEM((u3_t.shape[0], grid_w), BF16),
-                        pltpu.VMEM((rank_h, grid_h), BF16), pltpu.VMEM((4, rank_t, frames), BF16), link, link, link, link,
+                        pltpu.VMEM((rank_h, grid_h), BF16), pltpu.VMEM((rank_t, 4 * frames), BF16), link, link, link, link,
                         pltpu.VMEM((frames, groups, TILE, grid_h), BF16),
                         pltpu.VMEM((half, frames, rank_h), F32), pltpu.VMEM((half // 2, frames, rank_h), F32),
                         pltpu.VMEM((4, half // 2, frames, rank_h), BF16),
-                        pltpu.VMEM((4, frames, frames), F32), pltpu.VMEM((3, 4, piece, frames), F32),
+                        pltpu.VMEM((frames, 4 * frames), F32), pltpu.VMEM((3, piece, 4 * frames), F32),
                         pltpu.VMEM((piece, rank_t), F32), pltpu.VMEM((16, piece, rank_t), F32),
                         pltpu.SemaphoreType.REGULAR, pltpu.SemaphoreType.REGULAR, pltpu.SemaphoreType.DMA, pltpu.SemaphoreType.DMA,
                         dma(frames // TILE)] + [dma(SLOTS)] * 4 + [dma(3)] * 2 + [dma(frames // BATCH)] * 8 + [dma(3)] * 2
@@ -507,7 +507,8 @@
             full = g_part[r, quad_rows(at), :]
             for way in range(len(quads)):
                 full = full + g_recv[way, r]
-            power = power + jnp.dot(full.astype(BF16), u2_ref[r], preferred_element_type=F32)
+            rows = u2_ref[:, r * grid_h:(r + 1) * grid_h].astype(BF16)
+            power = power + lax.dot_general(full.astype(BF16), rows, NT, preferred_element_type=F32)
         p_send[...] = power
         p_all[slot16] = power
         for step in OTHERS:
@@ -539,7 +540,7 @@
         z_copy(g).wait()
 
 
-def width_part(at, z_ref, height_ref, u3_ref, new_ref, core_ref, energy_ref, u2_cols, y_send, y_recv, y_own, y_line, g_part, g_core, g_quad,
+def width_part(at, z_ref, height_ref, u3_ref, new_ref, core_ref, energy_ref, u3_rows, u2_cols, y_send, y_recv, y_own, y_line, g_part, g_core, g_quad,
                p_all, q_send, q_all, c_send, c_recv, e_send, e_all,
                a_ss, a_rs, r_ss, l_ss, b_rs, k_ss, k_rs, d_ss, d_rs, q_ss, q_rs, p_ss, p_rs, f_ss, f_rs, n_ss, n_rs, e_ss, e_rs, h_ss, h_rs):
     z, y, x, c = at["z"], at["y"], at["x"], at["c"]
@@ -552,6 +553,8 @@
     span = 4 * width
     rank_h = height_ref.shape[2]
     side_h = rank_h // 2
+    for index in range(SIZE["z"]):
+        u3_rows[index] = u3_ref[:, index * span:(index + 1) * span].astype(BF16)
     u2_cols[...] = jnp.zeros(u2_cols.shape, BF16)
     for s in range(sources):
         half = height_ref.shape[0] // 2
@@ -630,7 +633,7 @@
         for way in ways:
             d_copy(block, way).wait_recv()
             full = full + g_quad[way, block]
-        return jnp.dot(full.astype(BF16), u3_ref[block], preferred_element_type=F32)
+        return lax.dot_general(full.astype(BF16), u3_rows[block], NT, preferred_element_type=F32)
 
     def pass_on(block):
         @pl.when((block <= z) & (z < last))
@@ -798,7 +801,7 @@
               f32(2, rows, grid_h), f32(2, rows // 2, grid_h), f32(3, 2, piece, grid_h),
               bf16(groups, rank // 2, TILE, grid_h), f32(piece, rank_h), f32(16, piece, rank_h), one, one,
               dma(4)] + [dma(groups)] * 8 + [dma(3), dma(3), dma(COUNT), dma(16)]
-    wide = [bf16(2, 2 * PAD, grid_h), bf16(4, 2, cols, width), bf16(4, 2, cols, width), bf16(2, cols, 4 * width), bf16(4, cols, 2 * 4 * width),
+    wide = [bf16(4, rank_w, 4 * width), bf16(2, 2 * PAD, grid_h), bf16(4, 2, cols, width), bf16(4, 2, cols, width), bf16(2, cols, 4 * width), bf16(4, cols, 2 * 4 * width),
             f32(4, 4 * width, 4 * width), f32(4, 2 * width, 4 * width), f32(3, 4, small, 4 * width),
             f32(4, 2 * 4, small, rank_w), f32(TILE, rank_w), f32(COUNT, TILE, rank_w),
             f32(4, 2, fourth, cols), f32(2 * 4, fourth, cols), f32(TILE, 128), f32(COUNT, TILE, 128),
@@ -815,7 +818,7 @@
         scratch_shapes=[bf16(2, groups, rank // 2, TILE, grid_h)] + height + wide,
         compiler_params=pltpu.CompilerParams(collective_id=2, has_side_effects=True, vmem_limit_bytes=LIMIT),
         name="second_stage",
-    )(x_all, t_mat, new_time, u2.astype(BF16).reshape(2, grid_h, rank_h), u3.astype(BF16).reshape(4, 4 * width, rank_w))
+    )(x_all, t_mat, new_time, u2.T, u3.T)
 
 
 def solution(mesh):

time: 485 us -> 477 us (0.984)
  Pallas kernels: 472 us -> 467 us
where the time goes in v4:
time: 477 us; the launch traced here: 476 us
  Pallas kernels  467 us (98%)
  local copies, waits for them, and re-layouts  8.19 us (2%)
    pallas_call x1, Pallas kernels, first_stage(): pl.pallas_call(first_kernel, out_shape=(jax.ShapeDtypeStruct((half // TIL...  310 us
    pallas_call x1, Pallas kernels, second_stage(): pl.pallas_call(second_kernel, out_shape=(jax.ShapeDtypeStruct((16, piece,...  157 us

profile of v4, /device:TPU:0, one launch (start us, length us, event | category | flops | bytes accessed | tf_op | source)
XLA Modules:
  0.0 476.3 jit_solution(2898761548926350474)
XLA Ops:
  0.6 310.1 %first_stage.1 = (bf16[10,96,8,360]{3,2,1,0:T(8,128)(2,1)}, bf16[4,96,10,8,360]{4,3,2,1,0:T(8,128)(2,1)}, f32[16,24,48]{2,1,0:T(8,128)}) custom-call(bf16[96,320,360]{2,1,0:T(8,128)(2,1)} %bitcast.14, bf16[96,40,8,360]{3,2,1,0:T(8,128)(2,1)} %bitcast.15, f32[160,1280]{1,0:T(8,128)} %bitcast.16, f32[88,720]{1,0:T(8,128)} %bitcast.20, f32[48,384]{1,0:T(8,128)} %bitcast.26), custom_call_target="tpu_custom_call" | custom-call | tf_op jit(solution)/shard_map/first_stage/pallas_call | solution.py:353
  310.8 0.0 copy-start
  310.8 157.3 %second_stage.1 = (f32[16,48,88]{2,1,0:T(8,128)}, f32[4,8,40,160]{3,2,1,0:T(8,128)}, f32[2,40,288]{2,1,0:T(8,128)}, f32[8,128]{1,0:T(8,128)}) custom-call(bf16[4,96,10,8,360]{4,3,2,1,0:T(8,128)(2,1)} %get-tuple-element.13.x_hbm, bf16[10,96,8,360]{3,2,1,0:T(8,128)(2,1)} %get-tuple-element.14.t_ref, f32[384,48]{1,0:T(8,128)} %bitcast.22, f32[88,720]{1,0:T(8,128)} %bitcast.21, ...), custom_call_target="tpu_custom_call" | custom-call | tf_op jit(solution)/shard_map/second_stage/pallas_call | solution.py:810
  468.1 0.0 copy-done
  468.1 0.7 copy.18
  468.9 1.2 slice.11
  470.1 1.0 slice.12
  471.1 0.9 copy.20
  471.9 2.6 copy.19
  474.5 1.0 reshape.36
  475.6 0.7 copy.17
  (1 shorter events, 0.0 us)
Async XLA Ops:
  310.8 157.3 %copy-start = (f32[16,24,48]{2,1,0:T(8,128)S(1)}, f32[16,24,48]{2,1,0:T(8,128)}, u32[]{:S(2)}) copy-start(f32[16,24,48]{2,1,0:T(8,128)} %get-tuple-element.12) | copy-start | bytes 221188
